TPU v7x, 32 devices: a whole 2x2x4 slice. The times are simulated.
32 devices in a mesh: section: 2 (over y), gx: 4 (over z), gy: 4 (over x, core).
Axes of the slice: x: 2, y: 2, z: 4, core: 2. Of those that a mesh axis runs over, the one named last changes fastest.
Arguments:
- fields: float32 [2, 4, 64, 256, 1024], P('section', None, None, 'gx', 'gy'), may hold values from -6 to 6
- slot_pick: int32 [4], replicated, may hold values from 0 to 3, each once
- courant_x: float32 [64, 256, 1024], P(None, 'gx', 'gy'), may hold values from 0.05 to 0.3
- courant_y: float32 [64, 256, 1024], P(None, 'gx', 'gy'), may hold values from 0.05 to 0.3
- horiz_diff: float32 [64], replicated, may hold values from 0.01 to 0.05
- vert_diff: float32 [64], replicated, may hold values from 0.01 to 0.1
- precip_class: int32 [256, 1024], P('gx', 'gy'), may hold values from 0 to 3
- class_rates: float32 [4], replicated, may hold values from 0.05 to 0.6
- vent_cells: int32 [64], replicated, may hold values from 0 to 262143
- vent_rate: float32 [64], replicated, may hold values from 0.5 to 2
- profile: float32 [64], replicated, may hold values from 0.05 to 1
Outputs:
- window_fields: float32 [2, 64, 256, 1024], P('section', None, 'gx', 'gy')
- sensitivity: float32 [64], replicated
Inputs may be any that keep to these rules, and one draw needn't show every extreme that they name: `slot_pick`: each slot number appears once.
All inputs are finite; a program needn't handle non-finite values.
Results may differ from a plain program's by a relative error of at most 0.000088.
Values sent between devices are 32-bit elements; how exact they have to be, the bound alone decides.
No kernel may reach another device: no remote copies, remote signals or barrier semaphores. Data moves between devices by JAX's collectives and lax.ppermute only.
A program may use at most 192 MiB of HBM per device.

v0:
```python
import functools

import jax
import jax.numpy as jnp
from jax import lax
from jax.experimental import pallas as pl
from jax.experimental.pallas import tpu as pltpu
from jax.sharding import PartitionSpec as P

LANES = 128
SUBLANES = 8


def vmem():
    return pl.BlockSpec(memory_space=pltpu.VMEM)


def hbm():
    return pl.BlockSpec(memory_space=pltpu.HBM)


def neighbour(value, axis, by):
    size = lax.axis_size(axis)
    pairs = [(i, i + by) for i in range(size) if 0 <= i + by < size]
    return lax.ppermute(value, axis, pairs)


def doubling_steps():
    steps = []
    for axis in ("gx", "gy"):
        step = 1
        while step < lax.axis_size(axis):
            steps.append((axis, step))
            step *= 2
    return steps


def partner(value, axis, step):
    return lax.ppermute(value, axis, [(i, i ^ step) for i in range(lax.axis_size(axis))])


def inverse(conc):
    return 1.0 / (1.0 + conc * conc)


def wash(conc):
    return conc * conc * inverse(conc)


def slope(conc):
    inv = inverse(conc)
    return 2.0 * conc * inv * inv


def iotas(rows, cols):
    return (
        lax.broadcasted_iota(jnp.int32, (rows, cols), 0),
        lax.broadcasted_iota(jnp.int32, (rows, cols), 1),
    )


def wide(block, cols):
    return jnp.concatenate([block] * (cols // LANES), axis=1)


def lane_to(block, lane, target):
    return pltpu.roll(block, lax.rem(target - lane + 2 * LANES, LANES), 1)


def get_row(ref, r, lanes=slice(None)):
    base = pl.multiple_of((r // SUBLANES) * SUBLANES, SUBLANES)
    block = ref[pl.ds(base, SUBLANES), lanes]
    return pltpu.roll(block, lax.rem(SUBLANES - lax.rem(r, SUBLANES), SUBLANES), 0)[0:1]


def put_row(ref, r, value, lanes=slice(None)):
    base = pl.multiple_of((r // SUBLANES) * SUBLANES, SUBLANES)
    block = ref[pl.ds(base, SUBLANES), lanes]
    sub = lax.broadcasted_iota(jnp.int32, block.shape, 0)
    ref[pl.ds(base, SUBLANES), lanes] = jnp.where(sub == lax.rem(r, SUBLANES), value, block)


class Sides:
    def __init__(self, west, east, south, north):
        self.west, self.east, self.south, self.north = west, east, south, north


def level_coefs(adjoint, z, levels, horiz, vert):
    h = horiz[z]
    k = vert[z]
    if adjoint:
        above = vert[jnp.minimum(z + 1, levels - 1)]
        below = vert[jnp.maximum(z - 1, 0)]
    else:
        above = below = k
    above = jnp.where(z < levels - 1, above, 0.0)
    below = jnp.where(z > 0, below, 0.0)
    return h, k, above, below


def apply_plane(adjoint, z, levels, field, up, down, cu, cv, horiz, vert, sides):
    rows, cols = field.shape
    row, col = iotas(rows, cols)
    h, k, above, below = level_coefs(adjoint, z, levels, horiz, vert)
    if adjoint:
        to_east = (cu + h) * field
        to_north = (cv + h) * field
    else:
        to_east = to_north = h * field
    west = pltpu.roll(field, 1, 0)
    east = pltpu.roll(to_east, rows - 1, 0)
    south = pltpu.roll(field, 1, 1)
    north = pltpu.roll(to_north, cols - 1, 1)
    if sides is not None:
        west = jnp.where(row == 0, get_row(sides.west, z), west)
        east = jnp.where(row == rows - 1, get_row(sides.east, z), east)
        south = jnp.where(col == 0, wide(lane_to(sides.south[...], z, 0), cols), south)
        north = jnp.where(
            col == cols - 1, wide(lane_to(sides.north[...], z, LANES - 1), cols), north
        )
    diag = 1.0 - cu - cv - (4.0 * h + 2.0 * k)
    if adjoint:
        total = diag * field + h * (west + south) + east + north
    else:
        total = diag * field + (cu + h) * west + (cv + h) * south + east + north
    return total + above * up + below * down


def here_of(cells, v, dims):
    _, rows, cols, grid_y = dims
    x = cells[v] // grid_y - lax.axis_index("gx") * rows
    y = lax.rem(cells[v], grid_y) - lax.axis_index("gy") * cols
    return x, y, (x >= 0) & (x < rows) & (y >= 0) & (y < cols)


def gather_vents(cells, source, target, dims):
    levels = dims[0]
    _, lane = iotas(SUBLANES, LANES)

    def one(v, carry):
        x, y, here = here_of(cells, v, dims)

        @pl.when(here)
        def _():
            base = pl.multiple_of((y // LANES) * LANES, LANES)
            low = lax.rem(y, LANES)
            top = pl.multiple_of((x // SUBLANES) * SUBLANES, SUBLANES)
            got = jnp.zeros((SUBLANES, LANES), jnp.float32)
            for z in range(levels):
                block = source[z, pl.ds(top, SUBLANES), pl.ds(base, LANES)]
                got = jnp.where(lane == z, lane_to(block, low, z), got)
            got = pltpu.roll(got, lax.rem(SUBLANES - lax.rem(x, SUBLANES), SUBLANES), 0)[0:1]
            put_row(target, 2 * levels + v, got, slice(LANES, 2 * LANES))

        return carry

    lax.fori_loop(0, cells.shape[0], one, 0)


def gather_edges(source, target, dims):
    levels, rows, cols, _ = dims
    _, lane = iotas(rows, LANES)

    def group(i, columns):
        base = pl.multiple_of(i * SUBLANES, SUBLANES)
        for s in range(SUBLANES):
            z = base + s
            columns = jnp.where(lane == z, lane_to(source[z, :, 0:LANES], 0, z), columns)
            columns = jnp.where(
                lane == z + levels,
                lane_to(source[z, :, cols - LANES : cols], LANES - 1, z + levels),
                columns,
            )
        for top, row in ((0, 0), (levels, rows - 1)):
            lines = [source[base + s, row : row + 1, :] for s in range(SUBLANES)]
            at = pl.multiple_of(top + base, SUBLANES)
            target[pl.ds(at, SUBLANES), :] = jnp.concatenate(lines, axis=0)
        return columns

    zero = jnp.zeros((rows, LANES), jnp.float32)
    columns = lax.fori_loop(0, levels // SUBLANES, group, zero)
    target[2 * levels : 2 * levels + rows, 0:LANES] = columns


def head_kernel(slot_hbm, fields, out, slot, sems):
    copy = pltpu.make_async_copy(slot_hbm, slot, sems.at[0])
    copy.start()
    copy.wait()
    pick = slot[lax.axis_index("section")]
    copy = pltpu.make_async_copy(fields.at[0, pick, pl.ds(0, out.shape[0])], out, sems.at[1])
    copy.start()
    copy.wait()


def edges_kernel(
    dims,
    slot_hbm,
    horiz_hbm,
    class_hbm,
    cells_hbm,
    vent_hbm,
    fields,
    cu_hbm,
    cv_hbm,
    precip,
    out_xf,
    out_xb,
    out_yf,
    out_yb,
    out_cu0,
    out_cv0,
    out_rate,
    out_column,
    out_edges,
    out_edge_rate,
    slot,
    horiz,
    class_rates,
    cells,
    vent_rate,
    field,
    cu,
    cv,
    small_sems,
    sems,
):
    levels, rows, cols, _ = dims
    adj = lax.axis_index("section")
    flag = adj.astype(jnp.float32)
    courants = [
        pltpu.make_async_copy(cv_hbm.at[:, :, pl.ds(0, LANES)], cv, sems.at[1]),
        pltpu.make_async_copy(cu_hbm.at[:, pl.ds(0, SUBLANES), :], cu, sems.at[2]),
    ]
    small = [
        pltpu.make_async_copy(a, b, small_sems.at[i])
        for i, (a, b) in enumerate(
            (
                (slot_hbm, slot),
                (horiz_hbm, horiz),
                (class_hbm, class_rates),
                (cells_hbm, cells),
                (vent_hbm, vent_rate),
            )
        )
    ]
    for copy in small:
        copy.start()
    for copy in small:
        copy.wait()
    copies = [pltpu.make_async_copy(fields.at[0, slot[adj]], field, sems.at[0])] + courants
    for copy in copies:
        copy.start()

    kinds = precip[...]
    rate = jnp.zeros((rows, cols), jnp.float32)
    for kind in range(class_rates.shape[0]):
        rate = jnp.where(kinds == kind, class_rates[kind], rate)
    out_rate[...] = rate
    out_column[...] = jnp.zeros((rows, cols), jnp.float32)
    tail = slice(2 * levels, out_edges.shape[0])
    blank = jnp.zeros((out_edges.shape[0] - 2 * levels, cols), jnp.float32)
    out_edges[tail, :] = blank
    out_edge_rate[tail, :] = blank
    _, line_col = iotas(1, cols)

    def one(v, carry):
        x, y, here = here_of(cells, v, dims)

        @pl.when(here)
        def _():
            hit = line_col == y
            line = get_row(out_column, x) + jnp.where(hit, vent_rate[v], 0.0)
            put_row(out_column, x, line)
            found = jnp.sum(jnp.where(hit, get_row(out_rate, x), 0.0), axis=1, keepdims=True)
            found = jnp.broadcast_to(found, (1, LANES))
            put_row(out_edge_rate, 2 * levels + v, found, slice(LANES, 2 * LANES))

        return carry

    lax.fori_loop(0, cells.shape[0], one, 0)
    out_edge_rate[0:levels, :] = jnp.broadcast_to(rate[0:1, :], (levels, cols))
    out_edge_rate[levels : 2 * levels, :] = jnp.broadcast_to(rate[rows - 1 : rows, :], (levels, cols))
    _, lane = iotas(rows, LANES)
    out_edge_rate[2 * levels : 2 * levels + rows, 0:LANES] = jnp.where(
        lane < levels, rate[:, 0:1], rate[:, cols - 1 : cols]
    )

    copies[0].wait()
    gather_edges(field, out_edges, dims)
    gather_vents(cells, field, out_edges, dims)
    copies[1].wait()
    copies[2].wait()

    def group(i, columns):
        base = pl.multiple_of(i * SUBLANES, SUBLANES)
        lines = []
        for s in range(SUBLANES):
            z = base + s
            h = horiz[z]
            block = h + flag * cv[z]
            columns = jnp.where(lane == z, lane_to(block, 0, z), columns)
            lines.append(h + flag * cu[z, 0:1, :])
        out_cu0[pl.ds(base, SUBLANES), :] = jnp.concatenate(lines, axis=0)
        return columns

    zero = jnp.zeros((rows, LANES), jnp.float32)
    out_cv0[...] = lax.fori_loop(0, levels // SUBLANES, group, zero)
    columns = out_edges[2 * levels : 2 * levels + rows, 0:LANES]
    out_xf[...] = out_edges[levels : 2 * levels, :]
    out_xb[...] = out_cu0[...] * out_edges[0:levels, :]
    out_yf[...] = pltpu.roll(columns, LANES - levels, 1)
    out_yb[...] = out_cv0[...] * columns


def load_small(pairs, sems):
    copies = [pltpu.make_async_copy(a, b, sems.at[i]) for i, (a, b) in enumerate(pairs)]
    for copy in copies:
        copy.start()
    for copy in copies:
        copy.wait()


def first_kernel(
    dims,
    chunks,
    blocks,
    slot_hbm,
    horiz_hbm,
    vert_hbm,
    profile_hbm,
    cells_hbm,
    fields,
    cu_hbm,
    cv_hbm,
    west,
    east,
    south,
    north,
    rate,
    column,
    *rest,
):
    levels, _, cols, _ = dims
    out_pack, out_edges = rest[:2]
    out_chunks = rest[2 : 2 + len(chunks)]
    slot, horiz, vert, profile, cells = rest[2 + len(chunks) : 7 + len(chunks)]
    field, cu, cv, first, small_sems, in_sems, out_sems, chunk_sems = rest[7 + len(chunks) :]
    adj = lax.axis_index("section")
    size = levels // blocks
    spans = [pl.ds(b * size, size) for b in range(blocks)]
    loads = [
        [
            pltpu.make_async_copy(cu_hbm.at[span], cu.at[span], in_sems.at[b, 0]),
            pltpu.make_async_copy(cv_hbm.at[span], cv.at[span], in_sems.at[b, 1]),
        ]
        for b, span in enumerate(spans)
    ]
    for copy in loads[0]:
        copy.start()
    load_small(
        (
            (slot_hbm, slot),
            (horiz_hbm, horiz),
            (vert_hbm, vert),
            (profile_hbm, profile),
            (cells_hbm, cells),
        ),
        small_sems,
    )
    pick = slot[adj]
    for b, span in enumerate(spans):
        copy = pltpu.make_async_copy(fields.at[0, pick, span], field.at[span], in_sems.at[b, 2])
        copy.start()
        if b:
            for other in loads[b]:
                other.start()
        loads[b].append(copy)
    tail = slice(2 * levels, out_edges.shape[0])
    out_edges[tail, :] = jnp.zeros((out_edges.shape[0] - 2 * levels, cols), jnp.float32)
    sides = Sides(west, east, south, north)

    def planes(adjoint, low, high):
        def plane(z, carry):
            here = field[z]
            up = field[jnp.minimum(z + 1, levels - 1)]
            down = field[jnp.maximum(z - 1, 0)]
            value = apply_plane(
                adjoint, z, levels, here, up, down, cu[z], cv[z], horiz, vert, sides
            )
            if not adjoint:
                value = value - rate[...] * wash(here) + profile[z] * column[...]
            first[z] = value
            return carry

        lax.fori_loop(low, high, plane, 0)

    stores = []
    for copy in loads[0]:
        copy.wait()
    for b, span in enumerate(spans):
        if b + 1 < blocks:
            for copy in loads[b + 1]:
                copy.wait()
        low = b * size
        high = low + size

        @pl.when(adj == 0)
        def _():
            planes(False, low, high)

        @pl.when(adj == 1)
        def _():
            planes(True, low, high)

        for i, part in enumerate((first, cu, cv, field)):
            store = pltpu.make_async_copy(part.at[span], out_pack.at[span, i], out_sems.at[b, i])
            store.start()
            stores.append(store)
    for i, (low, high) in enumerate(chunks):
        span = pl.ds(low, high - low)
        store = pltpu.make_async_copy(field.at[span], out_chunks[i], chunk_sems.at[i])
        store.start()
        stores.append(store)
    gather_edges(first, out_edges, dims)
    gather_vents(cells, first, out_edges, dims)
    for store in stores:
        store.wait()


def rim_kernel(
    dims,
    profile,
    mine,
    theirs,
    edges,
    edge_rate,
    cu0,
    cv0,
    out_rim,
    out_xf,
    out_xb,
    out_yf,
    out_yb,
    out_terms,
):
    levels, rows, _, _ = dims
    adj = lax.axis_index("section")
    lam = mine[...] - edge_rate[...] * slope(theirs[...]) * edges[...]
    rim = jnp.where(adj == 1, lam, mine[...])
    out_rim[...] = rim
    columns = rim[2 * levels : 2 * levels + rows, 0:LANES]
    out_xf[...] = rim[levels : 2 * levels, :]
    out_xb[...] = cu0[...] * rim[0:levels, :]
    out_yf[...] = pltpu.roll(columns, LANES - levels, 1)
    out_yb[...] = cv0[...] * columns
    vents = out_terms.shape[1]
    at = slice(2 * levels, 2 * levels + vents)
    both = lam[at, LANES : 2 * LANES] + edges[at, LANES : 2 * LANES]
    weights = jnp.concatenate(
        [profile[...], jnp.zeros((1, LANES - levels), jnp.float32)], axis=1
    )
    both = jnp.concatenate([both * weights, jnp.zeros((LANES - vents, LANES), jnp.float32)], axis=0)
    sums = jnp.sum(jnp.transpose(both), axis=0, keepdims=True)[:, 0:vents]
    out_terms[...] = jnp.where(adj == 1, sums, 0.0)


def window_of(piece, levels):
    low, high = piece
    last = high == levels
    base = max(low - 3, 0)
    new0 = max(low - 1, 0)
    out0 = max(low - 2, 0)
    new1 = levels if last else high - 1
    out1 = levels if last else high - 2
    return base, (new0, new1), (out0, out1)


def load_kernel(base, pack, out, sem):
    copy = pltpu.make_async_copy(pack.at[pl.ds(base, out.shape[0])], out, sem.at[0])
    copy.start()
    copy.wait()


def chunk_kernel(
    dims,
    piece,
    following,
    horiz_hbm,
    vert_hbm,
    profile_hbm,
    pack,
    window,
    west,
    east,
    south,
    north,
    rate,
    column,
    rim,
    arrived,
    *rest,
):
    levels, rows, cols, _ = dims
    low, high = piece
    has_carry = low > 0
    if not following:
        terms, more_terms = rest[:2]
        rest = rest[2:]
    if has_carry:
        carry_in, _ = rest[:2]
        rest = rest[2:]
    out_hbm = rest[0]
    rest = rest[1:]
    if following:
        next_window, carry_out = rest[:2]
        rest = rest[2:]
    else:
        rest[0][...] = terms[...] + more_terms[...]
        rest = rest[1:]
    horiz, vert, profile, conc, fresh, result, small_sems, next_sem, out_sems = rest
    adj = lax.axis_index("section")
    base, (new0, new1), (out0, out1) = window_of(piece, levels)
    conc0 = out0
    sides = Sides(west, east, south, north)
    if following:
        start, _, _ = window_of(following, levels)
        ahead = pltpu.make_async_copy(
            pack.at[pl.ds(start, next_window.shape[0])], next_window, next_sem.at[0]
        )
        ahead.start()
    load_small(((horiz_hbm, horiz), (vert_hbm, vert), (profile_hbm, profile)), small_sems)

    def store(z):
        return pltpu.make_async_copy(
            result.at[z - out0], out_hbm.at[z], out_sems.at[z - out0]
        )

    @pl.when(adj == 1)
    def _():
        def move(z, carry):
            conc[low - conc0 + z] = arrived[z]
            return carry

        lax.fori_loop(0, high - low, move, 0)
        if has_carry:
            fresh[0:2] = carry_in[0:2]
            conc[0:2] = carry_in[2:4]

        def new_plane(z, carry):
            i = z - conc0
            j = z - base
            here = conc[i]
            up = conc[jnp.minimum(z + 1, levels - 1) - conc0]
            down = conc[jnp.maximum(z - 1, 0) - conc0]
            value = apply_plane(
                False, z, levels, here, up, down, window[j, 1], window[j, 2], horiz, vert, None
            )
            value = value - rate[...] * wash(here) + profile[z] * column[...]
            value = window[j, 0] - rate[...] * slope(value) * window[j, 3]
            row, col = iotas(rows, cols)
            columns = rim[2 * levels : 2 * levels + rows, 0:LANES]
            value = jnp.where(col == 0, wide(lane_to(columns, z, 0), cols), value)
            value = jnp.where(
                col == cols - 1, wide(lane_to(columns, z + levels, LANES - 1), cols), value
            )
            value = jnp.where(row == 0, get_row(rim, z), value)
            value = jnp.where(row == rows - 1, get_row(rim, levels + z), value)
            fresh[j] = value
            return carry

        lax.fori_loop(new0, new1, new_plane, 0)
        if following:
            carry_out[0:2] = fresh[new1 - 2 - base : new1 - base]
            carry_out[2:4] = conc[high - 2 - conc0 : high - conc0]

        def out_plane(z, carry):
            j = z - base
            here = fresh[j]
            up = fresh[jnp.minimum(z + 1, levels - 1) - base]
            down = fresh[jnp.maximum(z - 1, 0) - base]
            value = apply_plane(
                True, z, levels, here, up, down, window[j, 1], window[j, 2], horiz, vert, sides
            )
            result[z - out0] = value - rate[...] * slope(conc[z - conc0]) * here
            store(z).start()
            return carry

        lax.fori_loop(out0, out1, out_plane, 0)

    @pl.when(adj == 0)
    def _():
        def out_plane(z, carry):
            j = z - base
            here = window[j, 0]
            up = window[jnp.minimum(z + 1, levels - 1) - base, 0]
            down = window[jnp.maximum(z - 1, 0) - base, 0]
            value = apply_plane(
                False, z, levels, here, up, down, window[j, 1], window[j, 2], horiz, vert, sides
            )
            result[z - out0] = value - rate[...] * wash(here) + profile[z] * column[...]
            store(z).start()
            return carry

        lax.fori_loop(out0, out1, out_plane, 0)

    def wait(z, carry):
        store(z).wait()
        return carry

    lax.fori_loop(out0, out1, wait, 0)
    if following:
        ahead.wait()


def cost(cells, ops, arrays):
    return pl.CostEstimate(flops=cells * ops, bytes_accessed=4 * cells * arrays, transcendentals=0)


def cuts(levels):
    unit = levels // 16
    sizes = [5 * unit, 4 * unit, 4 * unit, 2 * unit, levels - 15 * unit]
    bounds = [0]
    for size in sizes:
        bounds.append(bounds[-1] + size)
    return list(zip(bounds[:-1], bounds[1:]))


def program(
    fields,
    slot_pick,
    courant_x,
    courant_y,
    horiz_diff,
    vert_diff,
    precip_class,
    class_rates,
    vent_cells,
    vent_rate,
    profile,
):
    levels, rows, cols = courant_x.shape
    vents = vent_cells.shape[0]
    grid_y = cols * lax.axis_size("gy")
    dims = (levels, rows, cols, grid_y)
    cells = levels * rows * cols
    edge_rows = 2 * levels + max(rows, vents)
    f32 = jnp.float32
    i32 = jnp.int32
    shape = jax.ShapeDtypeStruct
    full = shape((levels, rows, cols), f32)
    line = shape((levels, cols), f32)
    side = shape((rows, LANES), f32)
    flat = shape((rows, cols), f32)
    rims = shape((edge_rows, cols), f32)
    pieces = cuts(levels)

    whole_vmem = pltpu.CompilerParams(vmem_limit_bytes=58 * 1024 * 1024)
    params = pltpu.CompilerParams(vmem_limit_bytes=45 * 1024 * 1024)

    def send(value):
        return neighbour(value, "section", 1)

    low, high = pieces[0]
    start = pl.pallas_call(
        head_kernel,
        name="head",
        in_specs=[hbm()] * 2,
        out_specs=vmem(),
        out_shape=shape((high - low, rows, cols), f32),
        scratch_shapes=[pltpu.SMEM(slot_pick.shape, i32), pltpu.SemaphoreType.DMA((2,))],
        compiler_params=params,
        cost_estimate=cost(cells, 1, 1),
    )(slot_pick, fields)
    received = [send(start)]

    xf, xb, yf, yb, cu0, cv0, rate, column, edges, edge_rate = pl.pallas_call(
        functools.partial(edges_kernel, dims),
        name="edges",
        in_specs=[hbm()] * 8 + [vmem()],
        out_specs=[vmem()] * 10,
        out_shape=[line, line, side, side, line, side, flat, flat, rims, rims],
        scratch_shapes=[
            pltpu.SMEM(slot_pick.shape, i32),
            pltpu.SMEM(horiz_diff.shape, f32),
            pltpu.SMEM(class_rates.shape, f32),
            pltpu.SMEM(vent_cells.shape, i32),
            pltpu.SMEM(vent_rate.shape, f32),
            pltpu.VMEM(full.shape, f32),
            pltpu.VMEM((levels, SUBLANES, cols), f32),
            pltpu.VMEM((levels, rows, LANES), f32),
            pltpu.SemaphoreType.DMA((5,)),
            pltpu.SemaphoreType.DMA((3,)),
        ],
        compiler_params=whole_vmem,
        cost_estimate=cost(cells, 10, 2),
    )(
        slot_pick, horiz_diff, class_rates, vent_cells, vent_rate,
        fields, courant_x, courant_y, precip_class,
    )

    west = neighbour(xf, "gx", 1)
    east = neighbour(xb, "gx", -1)
    south = neighbour(yf, "gy", 1)
    north = neighbour(yb, "gy", -1)

    levels_smem = [pltpu.SMEM((levels,), f32)] * 3
    blocks = 4
    pack, mine, *later = pl.pallas_call(
        functools.partial(first_kernel, dims, pieces[1:], blocks),
        name="first",
        in_specs=[hbm()] * 8 + [vmem()] * 6,
        out_specs=[hbm(), vmem()] + [hbm()] * (len(pieces) - 1),
        out_shape=[shape((levels, 4, rows, cols), f32), rims]
        + [shape((b - a, rows, cols), f32) for a, b in pieces[1:]],
        scratch_shapes=[pltpu.SMEM(slot_pick.shape, i32)]
        + levels_smem
        + [pltpu.SMEM(vent_cells.shape, i32)]
        + [pltpu.VMEM(full.shape, f32)] * 4
        + [
            pltpu.SemaphoreType.DMA((5,)),
            pltpu.SemaphoreType.DMA((blocks, 3)),
            pltpu.SemaphoreType.DMA((blocks, 4)),
            pltpu.SemaphoreType.DMA((len(pieces) - 1,)),
        ],
        compiler_params=whole_vmem,
        cost_estimate=cost(cells, 40, 5),
    )(
        slot_pick, horiz_diff, vert_diff, profile, vent_cells,
        fields, courant_x, courant_y, west, east, south, north, rate, column,
    )

    theirs = send(mine)
    for piece in later:
        received.append(send(piece))

    rim, xf, xb, yf, yb, terms = pl.pallas_call(
        functools.partial(rim_kernel, dims),
        name="rim",
        in_specs=[vmem()] * 7,
        out_specs=[vmem()] * 6,
        out_shape=[rims, line, line, side, side, shape((1, vents), f32)],
        compiler_params=params,
        cost_estimate=cost(edge_rows * cols, 20, 5),
    )(profile[None, :], mine, theirs, edges, edge_rate, cu0, cv0)
    west = neighbour(xf, "gx", 1)
    east = neighbour(xb, "gx", -1)
    south = neighbour(yf, "gy", 1)
    north = neighbour(yb, "gy", -1)

    def load_window(piece):
        base, (_, end), _ = window_of(piece, levels)
        return shape((end - base, 4, rows, cols), f32)

    window = pl.pallas_call(
        functools.partial(load_kernel, window_of(pieces[0], levels)[0]),
        name="load",
        in_specs=[hbm()],
        out_specs=vmem(),
        out_shape=load_window(pieces[0]),
        scratch_shapes=[pltpu.SemaphoreType.DMA((1,))],
        compiler_params=params,
        cost_estimate=cost(cells, 10, 1),
    )(pack)

    terms = terms + lax.ppermute(terms, "section", [(1, 0)])
    steps = doubling_steps()
    while len(steps) > len(pieces) - 1:
        terms = terms + partner(terms, *steps.pop(0))

    result = carry = None
    more = jnp.zeros_like(terms)
    for j, piece in enumerate(pieces):
        low, high = piece
        following = pieces[j + 1] if j + 1 < len(pieces) else None
        base, (_, end), (out0, out1) = window_of(piece, levels)
        outs = out1 - out0
        if following and steps:
            more = partner(terms, *steps.pop(0))
        operands = [
            horiz_diff, vert_diff, profile, pack, window,
            west, east, south, north, rate, column, rim, received[j],
        ]
        specs = [hbm()] * 4 + [vmem()] * 9
        aliases = {}
        if not following:
            operands += [terms, more]
            specs += [vmem()] * 2
        if low > 0:
            operands += [carry, result]
            specs += [vmem(), hbm()]
            aliases = {len(operands) - 1: 0}
        out_shape = [full]
        out_specs = [hbm()]
        if following:
            out_shape += [load_window(following), shape((4, rows, cols), f32)]
            out_specs += [vmem(), vmem()]
        else:
            out_shape += [shape((1, vents), f32)]
            out_specs += [vmem()]
        result, *state = pl.pallas_call(
            functools.partial(chunk_kernel, dims, piece, following),
            in_specs=specs,
            out_specs=out_specs,
            out_shape=out_shape,
            scratch_shapes=levels_smem
            + [
                pltpu.VMEM((high - out0, rows, cols), f32),
                pltpu.VMEM((end - base, rows, cols), f32),
                pltpu.VMEM((outs, rows, cols), f32),
                pltpu.SemaphoreType.DMA((3,)),
                pltpu.SemaphoreType.DMA((1,)),
                pltpu.SemaphoreType.DMA((outs,)),
            ],
            input_output_aliases=aliases,
            compiler_params=params,
            cost_estimate=cost((high - low) * rows * cols, 80, 7),
        )(*operands)
        if following:
            window, carry = state
            if steps:
                terms = terms + more
                more = jnp.zeros_like(terms)
        else:
            (terms,) = state
    return (result[None], terms[0])


def solution(mesh):
    return jax.shard_map(
        program,
        mesh=mesh,
        in_specs=(
            P("section", None, None, "gx", "gy"),
            P(),
            P(None, "gx", "gy"),
            P(None, "gx", "gy"),
            P(),
            P(),
            P("gx", "gy"),
            P(),
            P(),
            P(),
            P(),
        ),
        out_specs=(P("section", None, "gx", "gy"), P()),
        check_vma=False,
    )
```

profile of v0, /device:TPU:12, one launch (start us, length us, event | category | flops | bytes accessed | tf_op | source)
XLA Modules:
  0.0 178.1 jit_solution(11407668401356962010)
XLA Ops:
  4.5 10.1 %edges.1 = (f32[64,256]{1,0:T(8,128)}, f32[64,256]{1,0:T(8,128)}, f32[64,128]{1,0:T(8,128)}, f32[64,128]{1,0:T(8,128)}, f32[64,256]{1,0:T(8,128)}, /*index=5*/f3...) custom-call(s32[4]{0:T(128)} %slot_hbm.5, f32[64]{0:T(128)} %horiz_hbm.13, ...), custom_call_target="tpu_custom_call" | custom-call | flops 10485760 | bytes 8388608 | tf_op jit(solution)/shard_map/edges/pallas_call | solution.py:676
  14.6 2.8 %collective-permute-start = (f32[64,256]{1,0:T(8,128)}, f32[64,256]{1,0:T(8,128)S(1)}, u32[]{:S(2)}, u32[]{:S(2)}) collective-permute-start(f32[64,256]{1,0:T(8,128)} %get-tuple-element.38), channel_id=1, source_target_pairs={{0,4},{4,8},{8,12},{1,5},{5,9},{9,13},{2,6},{6,10},{10,14},{3,7},{... | collective-permute-start | bytes 196616 | tf_op jit(solution)/shard_map/ppermute | solution.py:25
  17.4 3.1 %collective-permute-start.1 = (f32[64,256]{1,0:T(8,128)}, f32[64,256]{1,0:T(8,128)S(1)}, u32[]{:S(2)}, u32[]{:S(2)}) collective-permute-start(f32[64,256]{1,0:T(8,128)} %get-tuple-element.39), channel_id=1, source_target_pairs={{4,0},{8,4},{12,8},{5,1},{9,5},{13,9},{6,2},{10,6},{14,10},{7,3},{... | collective-permute-start | bytes 196616 | tf_op jit(solution)/shard_map/ppermute | solution.py:25
  23.1 3.2 %collective-permute-done.3.north = f32[64,128]{1,0:T(8,128)S(1)} collective-permute-done((f32[64,128]{1,0:T(8,128)}, f32[64,128]{1,0:T(8,128)S(1)}, u32[]{:S(2)}, u32[]{:S(2)}) %collective-permute-start.3) | collective-permute-done | bytes 32800 | tf_op jit(solution)/shard_map/ppermute | solution.py:25
  26.9 17.4 %first.1 = (f32[64,4,64,256]{3,2,1,0:T(8,128)}, f32[192,256]{1,0:T(8,128)}, f32[16,64,256]{2,1,0:T(8,128)}, f32[16,64,256]{2,1,0:T(8,128)}, f32[8,64,256]{2,1,0:T(8,128)}, /*index=5*/f32[4,64,256]{2,1,0:T(8,128)}) custom-call(s32[4]{0:T(128)} %slot_hbm.5, f32[64]{0:T(128)} %horiz_hbm.13, f32[64]{0:T(128)} %vert_hbm.11, f32[64]{0:T(128)} %profile_hbm.11, ...), custom_call_target="tpu_custom_call" | custom-call | flops 41943040 | bytes 20971520 | tf_op jit(solution)/shard_map/first/pallas_call | solution.py:708
  49.5 48.6 %collective-permute-done.4.theirs = f32[192,256]{1,0:T(8,128)S(1)} collective-permute-done((f32[192,256]{1,0:T(8,128)}, f32[192,256]{1,0:T(8,128)S(1)}, u32[]{:S(2)}, u32[]{:S(2)}) %collective-permute-start.4) | collective-permute-done | bytes 196640 | tf_op jit(solution)/shard_map/ppermute | solution.py:25
  102.1 3.6 %collective-permute-done.15 = f32[1,64]{1,0:T(1,128)S(1)} collective-permute-done((f32[1,64]{1,0:T(1,128)S(1)}, f32[1,64]{1,0:T(1,128)S(1)}, u32[]{:S(2)}, u32[]{:S(2)}) %collective-permute-start.15) | collective-permute-done | bytes 288 | tf_op jit(solution)/shard_map/ppermute | solution.py:39
  107.3 2.9 %collective-permute-done.16 = f32[1,64]{1,0:T(1,128)S(1)} collective-permute-done((f32[1,64]{1,0:T(1,128)S(1)}, f32[1,64]{1,0:T(1,128)S(1)}, u32[]{:S(2)}, u32[]{:S(2)}) %collective-permute-start.16) | collective-permute-done | bytes 288 | tf_op jit(solution)/shard_map/ppermute | solution.py:39
  111.3 2.1 %collective-permute-start.7 = (f32[64,128]{1,0:T(8,128)S(1)}, f32[64,128]{1,0:T(8,128)S(1)}, u32[]{:S(2)}, u32[]{:S(2)}) collective-permute-start(f32[64,128]{1,0:T(8,128)S(1)} %get-tuple-element.52), channel_id=1, source_target_pairs={{0,1},{1,2},{2,3},{4,5},{5,6},{6,7},{8,9},{9,10},{10,11},{12,13},{... | collective-permute-start | bytes 98312 | tf_op jit(solution)/shard_map/ppermute | solution.py:25
  115.5 4.9 %collective-permute-done.8.north = f32[64,128]{1,0:T(8,128)S(1)} collective-permute-done((f32[64,128]{1,0:T(8,128)S(1)}, f32[64,128]{1,0:T(8,128)S(1)}, u32[]{:S(2)}, u32[]{:S(2)}) %collective-permute-start.8) | collective-permute-done | bytes 32800 | tf_op jit(solution)/shard_map/ppermute | solution.py:25
  120.3 2.9 %collective-permute-start.5 = (f32[64,256]{1,0:T(8,128)S(1)}, f32[64,256]{1,0:T(8,128)S(1)}, u32[]{:S(2)}, u32[]{:S(2)}) collective-permute-start(f32[64,256]{1,0:T(8,128)S(1)} %get-tuple-element.50), channel_id=1, source_target_pairs={{0,4},{4,8},{8,12},{1,5},{5,9},{9,13},{2,6},{6,10},{10,14},{3,7},{... | collective-permute-start | bytes 196616 | tf_op jit(solution)/shard_map/ppermute | solution.py:25
  123.3 3.2 %collective-permute-done.5.west = f32[64,256]{1,0:T(8,128)S(1)} collective-permute-done((f32[64,256]{1,0:T(8,128)S(1)}, f32[64,256]{1,0:T(8,128)S(1)}, u32[]{:S(2)}, u32[]{:S(2)}) %collective-permute-start.5) | collective-permute-done | bytes 65568 | tf_op jit(solution)/shard_map/ppermute | solution.py:25
  126.5 1.9 %collective-permute-start.6 = (f32[64,256]{1,0:T(8,128)S(1)}, f32[64,256]{1,0:T(8,128)S(1)}, u32[]{:S(2)}, u32[]{:S(2)}) collective-permute-start(f32[64,256]{1,0:T(8,128)S(1)} %get-tuple-element.51), channel_id=1, source_target_pairs={{4,0},{8,4},{12,8},{5,1},{9,5},{13,9},{6,2},{10,6},{14,10},{7,3},{... | collective-permute-start | bytes 196616 | tf_op jit(solution)/shard_map/ppermute | solution.py:25
  128.4 4.2 %collective-permute-done.6.east = f32[64,256]{1,0:T(8,128)S(1)} collective-permute-done((f32[64,256]{1,0:T(8,128)S(1)}, f32[64,256]{1,0:T(8,128)S(1)}, u32[]{:S(2)}, u32[]{:S(2)}) %collective-permute-start.6) | collective-permute-done | bytes 65568 | tf_op jit(solution)/shard_map/ppermute | solution.py:25
  134.0 2.5 %load.1.window = f32[19,4,64,256]{3,2,1,0:T(8,128)S(1)} custom-call(f32[64,4,64,256]{3,2,1,0:T(8,128)} %get-tuple-element.44.pack), custom_call_target="tpu_custom_call" | custom-call | flops 10485760 | bytes 4194304 | tf_op jit(solution)/shard_map/load/pallas_call | solution.py:754
  136.5 2.2 %copy-done = f32[19,4,64,256]{3,2,1,0:T(8,128)} copy-done((f32[19,4,64,256]{3,2,1,0:T(8,128)}, f32[19,4,64,256]{3,2,1,0:T(8,128)S(1)}, u32[]{:S(2)}) %copy-start) | copy-done | bytes 4980760
  138.7 3.1 %collective-permute-start.18 = (f32[1,64]{1,0:T(1,128)S(1)}, f32[1,64]{1,0:T(1,128)S(1)}, u32[]{:S(2)}, u32[]{:S(2)}) collective-permute-start(f32[1,64]{1,0:T(1,128)S(1)} %add.15.rest_0_), channel_id=1, source_target_pairs={{0,2},{1,3},{2,0},{3,1},{4,6},{5,7},{6,4},{7,5},{8,10},{9,11},{10,... | collective-permute-start | bytes 776 | tf_op jit(solution)/shard_map/ppermute | solution.py:39
  141.8 8.9 %shard_map.122 = (f32[64,64,256]{2,1,0:T(8,128)}, f32[18,4,64,256]{3,2,1,0:T(8,128)S(1)}, f32[4,64,256]{2,1,0:T(8,128)S(1)}) custom-call(f32[64]{0:T(128)S(1)} %copy-done.10, f32[64]{0:T(128)S(1)} %copy-done.12, f32[64]{0:T(128)S(1)} %copy-done.11, f32[64,4,64,256]{3,2,1,0:T(8,128)} %get-tuple-element.44.pack, f32[19,4,64,256]{3,2,1,0:T(8,128)} %copy-done, ...), custom_call_target="tpu_custom_call" | custom-call | flops 26214400 | bytes 9175040 | tf_op jit(solution)/shard_map/pallas_call | solution.py:800
  150.7 2.1 %copy-done.2 = f32[18,4,64,256]{3,2,1,0:T(8,128)} copy-done((f32[18,4,64,256]{3,2,1,0:T(8,128)}, f32[18,4,64,256]{3,2,1,0:T(8,128)S(1)}, u32[]{:S(2)}) %copy-start.2) | copy-done | bytes 4718616
  152.8 8.1 %shard_map.123 = (f32[64,64,256]{2,1,0:T(8,128)}, f32[18,4,64,256]{3,2,1,0:T(8,128)S(1)}, f32[4,64,256]{2,1,0:T(8,128)S(1)}) custom-call(f32[64]{0:T(128)S(1)} %copy-done.10, f32[64]{0:T(128)S(1)} %copy-done.12, f32[64]{0:T(128)S(1)} %copy-done.11, f32[64,4,64,256]{3,2,1,0:T(8,128)} %get-tuple-element.44.pack, ...), custom_call_target="tpu_custom_call", output_to_operand_aliasing={{0}: (14, {})} | custom-call | flops 20971520 | bytes 7340032 | tf_op jit(solution)/shard_map/pallas_call | solution.py:800
  160.9 2.1 %copy-done.1 = f32[18,4,64,256]{3,2,1,0:T(8,128)} copy-done((f32[18,4,64,256]{3,2,1,0:T(8,128)}, f32[18,4,64,256]{3,2,1,0:T(8,128)S(1)}, u32[]{:S(2)}) %copy-start.1) | copy-done | bytes 4718616
  163.1 8.1 %shard_map.124 = (f32[64,64,256]{2,1,0:T(8,128)}, f32[10,4,64,256]{3,2,1,0:T(8,128)S(1)}, f32[4,64,256]{2,1,0:T(8,128)S(1)}) custom-call(f32[64]{0:T(128)S(1)} %copy-done.10, f32[64]{0:T(128)S(1)} %copy-done.12, f32[64]{0:T(128)S(1)} %copy-done.11, f32[64,4,64,256]{3,2,1,0:T(8,128)} %get-tuple-element.44.pack, ...), custom_call_target="tpu_custom_call", output_to_operand_aliasing={{0}: (14, {})} | custom-call | flops 20971520 | bytes 7340032 | tf_op jit(solution)/shard_map/pallas_call | solution.py:800
  171.2 3.5 %shard_map.125 = (f32[64,64,256]{2,1,0:T(8,128)}, f32[7,4,64,256]{3,2,1,0:T(8,128)S(1)}, f32[4,64,256]{2,1,0:T(8,128)S(1)}) custom-call(f32[64]{0:T(128)S(1)} %copy-done.10, f32[64]{0:T(128)S(1)} %copy-done.12, f32[64]{0:T(128)S(1)} %copy-done.11, f32[64,4,64,256]{3,2,1,0:T(8,128)} %get-tuple-element.44.pack, ...), custom_call_target="tpu_custom_call", output_to_operand_aliasing={{0}: (14, {})} | custom-call | flops 10485760 | bytes 3670016 | tf_op jit(solution)/shard_map/pallas_call | solution.py:800
  174.8 3.3 %shard_map.126 = (f32[64,64,256]{2,1,0:T(8,128)}, f32[1,64]{1,0:T(1,128)}) custom-call(f32[64]{0:T(128)S(1)} %copy-done.10, f32[64]{0:T(128)S(1)} %copy-done.12, f32[64]{0:T(128)S(1)} %copy-done.11, f32[64,4,64,256]{3,2,1,0:T(8,128)} %get-tuple-element.44.pack, f32[7,4,64,256]{3,2,1,0:T(8,128)S(1)} %get-tuple-element.67.window, ...), custom_call_target="tpu_custom_call", output_to_operand_aliasing={{0}: (16, {})} | custom-call | flops 5242880 | bytes 1835008 | tf_op jit(solution)/shard_map/pallas_call | solution.py:800
  (64 shorter events, 22.4 us)
Async XLA Ops:
  3.2 135.5 %collective-permute-start.9 = (f32[20,64,256]{2,1,0:T(8,128)S(1)}, f32[20,64,256]{2,1,0:T(8,128)S(1)}, u32[]{:S(2)}, u32[]{:S(2)}) collective-permute-start(f32[20,64,256]{2,1,0:T(8,128)S(1)} %head.1), channel_id=1, source_target_pairs={{0,16},{1,17},{2,18},{3,19},{4,20},{5,21},{6,22},{7,23},{8,24},{9,... | collective-permute-start | bytes 3932168 | tf_op jit(solution)/shard_map/ppermute | solution.py:25
  14.6 11.6 %collective-permute-start = (f32[64,256]{1,0:T(8,128)}, f32[64,256]{1,0:T(8,128)S(1)}, u32[]{:S(2)}, u32[]{:S(2)}) collective-permute-start(f32[64,256]{1,0:T(8,128)} %get-tuple-element.38), channel_id=1, source_target_pairs={{0,4},{4,8},{8,12},{1,5},{5,9},{9,13},{2,6},{6,10},{10,14},{3,7},{... | collective-permute-start | bytes 196616 | tf_op jit(solution)/shard_map/ppermute | solution.py:25
  17.4 8.8 %collective-permute-start.1 = (f32[64,256]{1,0:T(8,128)}, f32[64,256]{1,0:T(8,128)S(1)}, u32[]{:S(2)}, u32[]{:S(2)}) collective-permute-start(f32[64,256]{1,0:T(8,128)} %get-tuple-element.39), channel_id=1, source_target_pairs={{4,0},{8,4},{12,8},{5,1},{9,5},{13,9},{6,2},{10,6},{14,10},{7,3},{... | collective-permute-start | bytes 196616 | tf_op jit(solution)/shard_map/ppermute | solution.py:25
  20.4 2.6 %collective-permute-start.2 = (f32[64,128]{1,0:T(8,128)}, f32[64,128]{1,0:T(8,128)S(1)}, u32[]{:S(2)}, u32[]{:S(2)}) collective-permute-start(f32[64,128]{1,0:T(8,128)} %get-tuple-element.40), channel_id=1, source_target_pairs={{0,1},{1,2},{2,3},{4,5},{5,6},{6,7},{8,9},{9,10},{10,11},{12,13},{... | collective-permute-start | bytes 98312 | tf_op jit(solution)/shard_map/ppermute | solution.py:25
  21.7 4.5 %collective-permute-start.3 = (f32[64,128]{1,0:T(8,128)}, f32[64,128]{1,0:T(8,128)S(1)}, u32[]{:S(2)}, u32[]{:S(2)}) collective-permute-start(f32[64,128]{1,0:T(8,128)} %get-tuple-element.41), channel_id=1, source_target_pairs={{1,0},{2,1},{3,2},{5,4},{6,5},{7,6},{9,8},{10,9},{11,10},{13,12},{... | collective-permute-start | bytes 98312 | tf_op jit(solution)/shard_map/ppermute | solution.py:25
  26.9 71.2 %copy-start.5 = (f32[192,256]{1,0:T(8,128)S(1)}, f32[192,256]{1,0:T(8,128)}, u32[]{:S(2)}) copy-start(f32[192,256]{1,0:T(8,128)} %get-tuple-element.46.edges) | copy-start | bytes 589828
  26.9 71.2 %copy-start.6 = (f32[192,256]{1,0:T(8,128)S(1)}, f32[192,256]{1,0:T(8,128)}, u32[]{:S(2)}) copy-start(f32[192,256]{1,0:T(8,128)} %get-tuple-element.47.edge_rate) | copy-start | bytes 589828
  26.9 71.2 %copy-start.8 = (f32[64,256]{1,0:T(8,128)S(1)}, f32[64,256]{1,0:T(8,128)}, u32[]{:S(2)}) copy-start(f32[64,256]{1,0:T(8,128)} %get-tuple-element.48.cu0) | copy-start | bytes 196612
  26.9 71.2 %copy-start.9 = (f32[64,128]{1,0:T(8,128)S(1)}, f32[64,128]{1,0:T(8,128)}, u32[]{:S(2)}) copy-start(f32[64,128]{1,0:T(8,128)} %get-tuple-element.49.cv0) | copy-start | bytes 98308
  26.9 71.2 %copy-start.11 = (f32[64]{0:T(128)S(1)}, f32[64]{0:T(128)}, u32[]{:S(2)}) copy-start(f32[64]{0:T(128)} %profile_hbm.11) | copy-start | bytes 772
  44.3 108.5 %collective-permute-start.10 = (f32[16,64,256]{2,1,0:T(8,128)}, f32[16,64,256]{2,1,0:T(8,128)S(1)}, u32[]{:S(2)}, u32[]{:S(2)}) collective-permute-start(f32[16,64,256]{2,1,0:T(8,128)} %get-tuple-element.56), channel_id=1, source_target_pairs={{0,16},{1,17},{2,18},{3,19},{4,20},{5,21},{6,22},{7,23},{8,24},{9,... | collective-permute-start | bytes 3145736 | tf_op jit(solution)/shard_map/ppermute | solution.py:25
  45.6 117.4 %collective-permute-start.11 = (f32[16,64,256]{2,1,0:T(8,128)}, f32[16,64,256]{2,1,0:T(8,128)S(1)}, u32[]{:S(2)}, u32[]{:S(2)}) collective-permute-start(f32[16,64,256]{2,1,0:T(8,128)} %get-tuple-element.60), channel_id=1, source_target_pairs={{0,16},{1,17},{2,18},{3,19},{4,20},{5,21},{6,22},{7,23},{8,24},{9,... | collective-permute-start | bytes 3145736 | tf_op jit(solution)/shard_map/ppermute | solution.py:25
  46.9 51.2 %collective-permute-start.4 = (f32[192,256]{1,0:T(8,128)}, f32[192,256]{1,0:T(8,128)S(1)}, u32[]{:S(2)}, u32[]{:S(2)}) collective-permute-start(f32[192,256]{1,0:T(8,128)} %get-tuple-element.45.mine), channel_id=1, source_target_pairs={{0,16},{1,17},{2,18},{3,19},{4,20},{5,21},{6,22},{7,23},{8,24},{9,... | collective-permute-start | bytes 589832 | tf_op jit(solution)/shard_map/ppermute | solution.py:25
  48.2 122.9 %collective-permute-start.12 = (f32[8,64,256]{2,1,0:T(8,128)}, f32[8,64,256]{2,1,0:T(8,128)S(1)}, u32[]{:S(2)}, u32[]{:S(2)}) collective-permute-start(f32[8,64,256]{2,1,0:T(8,128)} %get-tuple-element.64), channel_id=1, source_target_pairs={{0,16},{1,17},{2,18},{3,19},{4,20},{5,21},{6,22},{7,23},{8,24},{9,... | collective-permute-start | bytes 1572872 | tf_op jit(solution)/shard_map/ppermute | solution.py:25
  99.2 2.8 %collective-permute-start.14 = (f32[1,64]{1,0:T(1,128)S(1)}, f32[1,64]{1,0:T(1,128)S(1)}, u32[]{:S(2)}, u32[]{:S(2)}) collective-permute-start(f32[1,64]{1,0:T(1,128)S(1)} %get-tuple-element.69), channel_id=1, source_target_pairs={{16,0},{17,1},{18,2},{19,3},{20,4},{21,5},{22,6},{23,7},{24,8},{25... | collective-permute-start | bytes 776 | tf_op jit(solution)/shard_map/ppermute | solution.py:765
  102.1 3.6 %collective-permute-start.15 = (f32[1,64]{1,0:T(1,128)S(1)}, f32[1,64]{1,0:T(1,128)S(1)}, u32[]{:S(2)}, u32[]{:S(2)}) collective-permute-start(f32[1,64]{1,0:T(1,128)S(1)} %add.12), channel_id=1, source_target_pairs={{0,4},{4,0},{8,12},{12,8},{1,5},{5,1},{9,13},{13,9},{2,6},{6,2},{1... | collective-permute-start | bytes 776 | tf_op jit(solution)/shard_map/ppermute | solution.py:39
  105.7 4.5 %collective-permute-start.16 = (f32[1,64]{1,0:T(1,128)S(1)}, f32[1,64]{1,0:T(1,128)S(1)}, u32[]{:S(2)}, u32[]{:S(2)}) collective-permute-start(f32[1,64]{1,0:T(1,128)S(1)} %add.13), channel_id=1, source_target_pairs={{0,8},{4,12},{8,0},{12,4},{1,9},{5,13},{9,1},{13,5},{2,10},{6,14},... | collective-permute-start | bytes 776 | tf_op jit(solution)/shard_map/ppermute | solution.py:39
  110.1 1.2 collective-permute-start.17
  111.3 2.9 %collective-permute-start.7 = (f32[64,128]{1,0:T(8,128)S(1)}, f32[64,128]{1,0:T(8,128)S(1)}, u32[]{:S(2)}, u32[]{:S(2)}) collective-permute-start(f32[64,128]{1,0:T(8,128)S(1)} %get-tuple-element.52), channel_id=1, source_target_pairs={{0,1},{1,2},{2,3},{4,5},{5,6},{6,7},{8,9},{9,10},{10,11},{12,13},{... | collective-permute-start | bytes 98312 | tf_op jit(solution)/shard_map/ppermute | solution.py:25
  114.2 6.1 %collective-permute-start.8 = (f32[64,128]{1,0:T(8,128)S(1)}, f32[64,128]{1,0:T(8,128)S(1)}, u32[]{:S(2)}, u32[]{:S(2)}) collective-permute-start(f32[64,128]{1,0:T(8,128)S(1)} %get-tuple-element.53), channel_id=1, source_target_pairs={{1,0},{2,1},{3,2},{5,4},{6,5},{7,6},{9,8},{10,9},{11,10},{13,12},{... | collective-permute-start | bytes 98312 | tf_op jit(solution)/shard_map/ppermute | solution.py:25
  120.3 6.1 %collective-permute-start.5 = (f32[64,256]{1,0:T(8,128)S(1)}, f32[64,256]{1,0:T(8,128)S(1)}, u32[]{:S(2)}, u32[]{:S(2)}) collective-permute-start(f32[64,256]{1,0:T(8,128)S(1)} %get-tuple-element.50), channel_id=1, source_target_pairs={{0,4},{4,8},{8,12},{1,5},{5,9},{9,13},{2,6},{6,10},{10,14},{3,7},{... | collective-permute-start | bytes 196616 | tf_op jit(solution)/shard_map/ppermute | solution.py:25
  126.5 6.1 %collective-permute-start.6 = (f32[64,256]{1,0:T(8,128)S(1)}, f32[64,256]{1,0:T(8,128)S(1)}, u32[]{:S(2)}, u32[]{:S(2)}) collective-permute-start(f32[64,256]{1,0:T(8,128)S(1)} %get-tuple-element.51), channel_id=1, source_target_pairs={{4,0},{8,4},{12,8},{5,1},{9,5},{13,9},{6,2},{10,6},{14,10},{7,3},{... | collective-permute-start | bytes 196616 | tf_op jit(solution)/shard_map/ppermute | solution.py:25
  132.6 42.1 %collective-permute-start.13 = (f32[4,64,256]{2,1,0:T(8,128)}, f32[4,64,256]{2,1,0:T(8,128)S(1)}, u32[]{:S(2)}, u32[]{:S(2)}) collective-permute-start(f32[4,64,256]{2,1,0:T(8,128)} %get-tuple-element.68), channel_id=1, source_target_pairs={{0,16},{1,17},{2,18},{3,19},{4,20},{5,21},{6,22},{7,23},{8,24},{9,... | collective-permute-start | bytes 786440 | tf_op jit(solution)/shard_map/ppermute | solution.py:25
  138.7 36.0 %collective-permute-start.18 = (f32[1,64]{1,0:T(1,128)S(1)}, f32[1,64]{1,0:T(1,128)S(1)}, u32[]{:S(2)}, u32[]{:S(2)}) collective-permute-start(f32[1,64]{1,0:T(1,128)S(1)} %add.15.rest_0_), channel_id=1, source_target_pairs={{0,2},{1,3},{2,0},{3,1},{4,6},{5,7},{6,4},{7,5},{8,10},{9,11},{10,... | collective-permute-start | bytes 776 | tf_op jit(solution)/shard_map/ppermute | solution.py:39
  (13 other events, 44.8 us)
where the time goes:
time: 179 us; the launch traced here: 178 us
  waiting for transfers between devices  73.7 us (41%)
  Pallas kernels  63.9 us (36%)
  starting transfers between devices  30.6 us (17%)
  local copies, waits for them, and re-layouts  8.8 us (5%)
    ppermute x14, waiting for transfers between devices, neighbour(): return lax.ppermute(value, axis, pairs)  64.9 us
    pallas_call x5, Pallas kernels, program(): pl.pallas_call(functools.partial(chunk_kernel, dims, piece, following), i...  31.9 us
    ppermute x14, starting transfers between devices, neighbour(): return lax.ppermute(value, axis, pairs)  24.3 us
    pallas_call x1, Pallas kernels, program(): pl.pallas_call(functools.partial(first_kernel, dims, pieces[1:], blocks),...  17.4 us
    pallas_call x1, Pallas kernels, program(): pl.pallas_call(functools.partial(edges_kernel, dims), name='edges', in_sp...  10.1 us
    unnamed x36, local copies, waits for them, and re-layouts  8.8 us
    ppermute x4, waiting for transfers between devices, partner(): lax.ppermute(value, axis, [(i, i ^ step) for i in range(lax.axis_size(axi...  7.55 us
    ppermute x4, starting transfers between devices, partner(): lax.ppermute(value, axis, [(i, i ^ step) for i in range(lax.axis_size(axi...  4.75 us
  transfers between devices with their start and end apart: 19, of which 10 were waited for; matrix products, arithmetic and copies ran while one was open for 0% of the time, Pallas kernels for 33%

commit v1 on v0

--- a/solution.py
+++ b/solution.py
@@ -9,6 +9,7 @@
 
 LANES = 128
 SUBLANES = 8
+SLOTS = 7
 
 
 def vmem():
@@ -26,17 +27,17 @@
 
 
 def doubling_steps():
+    wide, deep = lax.axis_size("gx"), lax.axis_size("gy")
     steps = []
-    for axis in ("gx", "gy"):
-        step = 1
-        while step < lax.axis_size(axis):
-            steps.append((axis, step))
-            step *= 2
+    step = 1
+    while step < wide * deep:
+        steps.append([(i, i ^ step) for i in range(wide * deep)])
+        step *= 2
     return steps
 
 
-def partner(value, axis, step):
-    return lax.ppermute(value, axis, [(i, i ^ step) for i in range(lax.axis_size(axis))])
+def partner(value, pairs):
+    return lax.ppermute(value, ("section", "gx", "gy"), pairs)
 
 
 def inverse(conc):
@@ -338,13 +339,14 @@
     north,
     rate,
     column,
+    edges,
     *rest,
 ):
     levels, _, cols, _ = dims
-    out_pack, out_edges = rest[:2]
-    out_chunks = rest[2 : 2 + len(chunks)]
-    slot, horiz, vert, profile, cells = rest[2 + len(chunks) : 7 + len(chunks)]
-    field, cu, cv, first, small_sems, in_sems, out_sems, chunk_sems = rest[7 + len(chunks) :]
+    out_pack, out_edges, out_vents = rest[:3]
+    out_chunks = rest[3 : 3 + len(chunks)]
+    slot, horiz, vert, profile, cells = rest[3 + len(chunks) : 8 + len(chunks)]
+    field, cu, cv, first, small_sems, in_sems, out_sems, chunk_sems = rest[8 + len(chunks) :]
     adj = lax.axis_index("section")
     size = levels // blocks
     spans = [pl.ds(b * size, size) for b in range(blocks)]
@@ -423,6 +425,9 @@
         stores.append(store)
     gather_edges(first, out_edges, dims)
     gather_vents(cells, first, out_edges, dims)
+    at = slice(2 * levels, 2 * levels + out_vents.shape[0])
+    out_vents[:, 0:LANES] = out_edges[at, LANES : 2 * LANES]
+    out_vents[:, LANES : 2 * LANES] = edges[at, LANES : 2 * LANES]
     for store in stores:
         store.wait()
 
@@ -432,6 +437,7 @@
     profile,
     mine,
     theirs,
+    at_vents,
     edges,
     edge_rate,
     cu0,
@@ -455,13 +461,16 @@
     out_yb[...] = cv0[...] * columns
     vents = out_terms.shape[1]
     at = slice(2 * levels, 2 * levels + vents)
-    both = lam[at, LANES : 2 * LANES] + edges[at, LANES : 2 * LANES]
+    right = slice(LANES, 2 * LANES)
+    lam_two = at_vents[:, right]
+    loss = edge_rate[at, right] * slope(mine[at, right]) * lam_two
+    both = at_vents[:, 0:LANES] - loss + lam_two
     weights = jnp.concatenate(
         [profile[...], jnp.zeros((1, LANES - levels), jnp.float32)], axis=1
     )
     both = jnp.concatenate([both * weights, jnp.zeros((LANES - vents, LANES), jnp.float32)], axis=0)
     sums = jnp.sum(jnp.transpose(both), axis=0, keepdims=True)[:, 0:vents]
-    out_terms[...] = jnp.where(adj == 1, sums, 0.0)
+    out_terms[...] = sums
 
 
 def window_of(piece, levels):
@@ -476,7 +485,9 @@
 
 
 def load_kernel(base, pack, out, sem):
-    copy = pltpu.make_async_copy(pack.at[pl.ds(base, out.shape[0])], out, sem.at[0])
+    copy = pltpu.make_async_copy(
+        pack.at[pl.ds(base, out.shape[0]), pl.ds(0, 4)], out, sem.at[0]
+    )
     copy.start()
     copy.wait()
 
@@ -515,7 +526,7 @@
         next_window, carry_out = rest[:2]
         rest = rest[2:]
     else:
-        rest[0][...] = terms[...] + more_terms[...]
+        rest[0][...] = jnp.where(lax.axis_index("section") == 1, more_terms[...], terms[...])
         rest = rest[1:]
     horiz, vert, profile, conc, fresh, result, small_sems, next_sem, out_sems = rest
     adj = lax.axis_index("section")
@@ -525,7 +536,7 @@
     if following:
         start, _, _ = window_of(following, levels)
         ahead = pltpu.make_async_copy(
-            pack.at[pl.ds(start, next_window.shape[0])], next_window, next_sem.at[0]
+            pack.at[pl.ds(start, next_window.shape[0]), pl.ds(0, 4)], next_window, next_sem.at[0]
         )
         ahead.start()
     load_small(((horiz_hbm, horiz), (vert_hbm, vert), (profile_hbm, profile)), small_sems)
@@ -617,8 +628,8 @@
 
 
 def cuts(levels):
-    unit = levels // 16
-    sizes = [5 * unit, 4 * unit, 4 * unit, 2 * unit, levels - 15 * unit]
+    sizes = [levels * part // 64 for part in (28, 16, 12, 6)]
+    sizes.append(levels - sum(sizes))
     bounds = [0]
     for size in sizes:
         bounds.append(bounds[-1] + size)
@@ -655,7 +666,8 @@
     pieces = cuts(levels)
 
     whole_vmem = pltpu.CompilerParams(vmem_limit_bytes=58 * 1024 * 1024)
-    params = pltpu.CompilerParams(vmem_limit_bytes=45 * 1024 * 1024)
+    params = pltpu.CompilerParams(vmem_limit_bytes=34 * 1024 * 1024)
+    head_params = pltpu.CompilerParams(vmem_limit_bytes=45 * 1024 * 1024)
 
     def send(value):
         return neighbour(value, "section", 1)
@@ -668,7 +680,7 @@
         out_specs=vmem(),
         out_shape=shape((high - low, rows, cols), f32),
         scratch_shapes=[pltpu.SMEM(slot_pick.shape, i32), pltpu.SemaphoreType.DMA((2,))],
-        compiler_params=params,
+        compiler_params=head_params,
         cost_estimate=cost(cells, 1, 1),
     )(slot_pick, fields)
     received = [send(start)]
@@ -705,12 +717,12 @@
 
     levels_smem = [pltpu.SMEM((levels,), f32)] * 3
     blocks = 4
-    pack, mine, *later = pl.pallas_call(
+    pack, mine, at_vents, *later = pl.pallas_call(
         functools.partial(first_kernel, dims, pieces[1:], blocks),
         name="first",
-        in_specs=[hbm()] * 8 + [vmem()] * 6,
-        out_specs=[hbm(), vmem()] + [hbm()] * (len(pieces) - 1),
-        out_shape=[shape((levels, 4, rows, cols), f32), rims]
+        in_specs=[hbm()] * 8 + [vmem()] * 7,
+        out_specs=[hbm(), vmem(), vmem()] + [hbm()] * (len(pieces) - 1),
+        out_shape=[shape((levels, SLOTS, rows, cols), f32), rims, shape((vents, 2 * LANES), f32)]
         + [shape((b - a, rows, cols), f32) for a, b in pieces[1:]],
         scratch_shapes=[pltpu.SMEM(slot_pick.shape, i32)]
         + levels_smem
@@ -726,22 +738,23 @@
         cost_estimate=cost(cells, 40, 5),
     )(
         slot_pick, horiz_diff, vert_diff, profile, vent_cells,
-        fields, courant_x, courant_y, west, east, south, north, rate, column,
+        fields, courant_x, courant_y, west, east, south, north, rate, column, edges,
     )
 
     theirs = send(mine)
+    at_vents = neighbour(at_vents, "section", -1)
     for piece in later:
         received.append(send(piece))
 
     rim, xf, xb, yf, yb, terms = pl.pallas_call(
         functools.partial(rim_kernel, dims),
         name="rim",
-        in_specs=[vmem()] * 7,
+        in_specs=[vmem()] * 8,
         out_specs=[vmem()] * 6,
         out_shape=[rims, line, line, side, side, shape((1, vents), f32)],
         compiler_params=params,
         cost_estimate=cost(edge_rows * cols, 20, 5),
-    )(profile[None, :], mine, theirs, edges, edge_rate, cu0, cv0)
+    )(profile[None, :], mine, theirs, at_vents, edges, edge_rate, cu0, cv0)
     west = neighbour(xf, "gx", 1)
     east = neighbour(xb, "gx", -1)
     south = neighbour(yf, "gy", 1)
@@ -762,20 +775,20 @@
         cost_estimate=cost(cells, 10, 1),
     )(pack)
 
-    terms = terms + lax.ppermute(terms, "section", [(1, 0)])
     steps = doubling_steps()
-    while len(steps) > len(pieces) - 1:
-        terms = terms + partner(terms, *steps.pop(0))
+    while len(steps) > 2:
+        terms = terms + partner(terms, steps.pop(0))
 
     result = carry = None
-    more = jnp.zeros_like(terms)
     for j, piece in enumerate(pieces):
         low, high = piece
         following = pieces[j + 1] if j + 1 < len(pieces) else None
         base, (_, end), (out0, out1) = window_of(piece, levels)
         outs = out1 - out0
-        if following and steps:
-            more = partner(terms, *steps.pop(0))
+        if steps:
+            more = partner(terms, steps.pop(0))
+        elif j == 2:
+            passed = neighbour(terms, "section", 1)
         operands = [
             horiz_diff, vert_diff, profile, pack, window,
             west, east, south, north, rate, column, rim, received[j],
@@ -783,7 +796,7 @@
         specs = [hbm()] * 4 + [vmem()] * 9
         aliases = {}
         if not following:
-            operands += [terms, more]
+            operands += [terms, passed]
             specs += [vmem()] * 2
         if low > 0:
             operands += [carry, result]
@@ -817,9 +830,8 @@
         )(*operands)
         if following:
             window, carry = state
-            if steps:
+            if j < 2:
                 terms = terms + more
-                more = jnp.zeros_like(terms)
         else:
             (terms,) = state
     return (result[None], terms[0])

time: 179 us -> 159 us (0.89)
  the two profiles are of different devices: /device:TPU:12 before, /device:TPU:0 now
where the time goes in v1:
time: 159 us; the launch traced here: 157 us
  waiting for transfers between devices  58.1 us (37%)
  starting transfers between devices  48.7 us (31%)
  Pallas kernels  47.3 us (30%)
  local copies, waits for them, and re-layouts  2.25 us (1%)
    ppermute x16, waiting for transfers between devices, neighbour(): return lax.ppermute(value, axis, pairs)  51.8 us
    ppermute x16, starting transfers between devices, neighbour(): return lax.ppermute(value, axis, pairs)  30.5 us
    ppermute x4, starting transfers between devices, partner(): return lax.ppermute(value, ('section', 'gx', 'gy'), pairs)  18.2 us
    pallas_call x1, Pallas kernels, program(): pl.pallas_call(functools.partial(first_kernel, dims, pieces[1:], blocks),...  17 us
    pallas_call x5, Pallas kernels, program(): pl.pallas_call(functools.partial(chunk_kernel, dims, piece, following), i...  15.8 us
    pallas_call x1, Pallas kernels, program(): pl.pallas_call(functools.partial(edges_kernel, dims), name='edges', in_sp...  9.26 us
    ppermute x4, waiting for transfers between devices, partner(): return lax.ppermute(value, ('section', 'gx', 'gy'), pairs)  6.38 us
  transfers between devices with their start and end apart: 20, of which 11 were waited for; matrix products, arithmetic and copies ran while one was open for 0% of the time, Pallas kernels for 27%

profile of v1, /device:TPU:0, one launch (start us, length us, event | category | flops | bytes accessed | tf_op | source)
XLA Modules:
  0.0 157.4 jit_solution(4720245843160384960)
XLA Ops:
  1.3 2.1 %head.1 = f32[28,64,256]{2,1,0:T(8,128)S(1)} custom-call(s32[4]{0:T(128)S(1)} %copy-done.10, f32[1,4,64,64,256]{4,3,2,1,0:T(8,128)} %fields.5), custom_call_target="tpu_custom_call" | custom-call | flops 1048576 | bytes 4194304 | tf_op jit(solution)/shard_map/head/pallas_call | solution.py:676
  3.4 5.0 %collective-permute-start.10 = (f32[28,64,256]{2,1,0:T(8,128)S(1)}, f32[28,64,256]{2,1,0:T(8,128)S(1)}, u32[]{:S(2)}, u32[]{:S(2)}) collective-permute-start(f32[28,64,256]{2,1,0:T(8,128)S(1)} %head.1), channel_id=1, source_target_pairs={{0,16},{1,17},{2,18},{3,19},{4,20},{5,21},{6,22},{7,23},{8,24},{9,... | collective-permute-start | bytes 5505032 | tf_op jit(solution)/shard_map/ppermute | solution.py:26
  8.4 9.3 %edges.1 = (f32[64,256]{1,0:T(8,128)}, f32[64,256]{1,0:T(8,128)}, f32[64,128]{1,0:T(8,128)}, f32[64,128]{1,0:T(8,128)}, f32[64,256]{1,0:T(8,128)}, /*index=5*/f3...) custom-call(s32[4]{0:T(128)} %slot_hbm.5, f32[64]{0:T(128)} %horiz_hbm.13, ...), custom_call_target="tpu_custom_call" | custom-call | flops 10485760 | bytes 8388608 | tf_op jit(solution)/shard_map/edges/pallas_call | solution.py:688
  17.7 4.3 %collective-permute-start = (f32[64,256]{1,0:T(8,128)}, f32[64,256]{1,0:T(8,128)S(1)}, u32[]{:S(2)}, u32[]{:S(2)}) collective-permute-start(f32[64,256]{1,0:T(8,128)} %get-tuple-element.39), channel_id=1, source_target_pairs={{0,4},{4,8},{8,12},{1,5},{5,9},{9,13},{2,6},{6,10},{10,14},{3,7},{... | collective-permute-start | bytes 196616 | tf_op jit(solution)/shard_map/ppermute | solution.py:26
  25.9 3.2 %collective-permute-done.3.north = f32[64,128]{1,0:T(8,128)S(1)} collective-permute-done((f32[64,128]{1,0:T(8,128)}, f32[64,128]{1,0:T(8,128)S(1)}, u32[]{:S(2)}, u32[]{:S(2)}) %collective-permute-start.3) | collective-permute-done | bytes 32800 | tf_op jit(solution)/shard_map/ppermute | solution.py:26
  29.7 17.0 %first.1 = (f32[64,7,64,256]{3,2,1,0:T(8,128)}, f32[192,256]{1,0:T(8,128)}, f32[64,256]{1,0:T(8,128)}, f32[16,64,256]{2,1,0:T(8,128)}, f32[12,64,256]{2,1,0:T(8,...) custom-call(s32[4]{0:T(128)} %slot_hbm.5, f32[64]{0:T(128)} %horiz_hbm.13, f32[64]{0:T(128)} %vert_hbm.11, ...), custom_call_target="tpu_custom_call" | custom-call | flops 41943040 | bytes 20971520 | tf_op jit(solution)/shard_map/first/pallas_call | solution.py:720
  52.0 5.1 %collective-permute-done.5.at_vents = f32[64,256]{1,0:T(8,128)S(1)} collective-permute-done((f32[64,256]{1,0:T(8,128)}, f32[64,256]{1,0:T(8,128)S(1)}, u32[]{:S(2)}, u32[]{:S(2)}) %collective-permute-start.5) | collective-permute-done | bytes 65568 | tf_op jit(solution)/shard_map/ppermute | solution.py:26
  58.8 32.5 %collective-permute-done.4.theirs = f32[192,256]{1,0:T(8,128)S(1)} collective-permute-done((f32[192,256]{1,0:T(8,128)}, f32[192,256]{1,0:T(8,128)S(1)}, u32[]{:S(2)}, u32[]{:S(2)}) %collective-permute-start.4) | collective-permute-done | bytes 196640 | tf_op jit(solution)/shard_map/ppermute | solution.py:26
  92.4 5.3 %collective-permute-start.15 = (f32[1,64]{1,0:T(1,128)S(1)}, f32[1,64]{1,0:T(1,128)S(1)}, u32[]{:S(2)}, u32[]{:S(2)}) collective-permute-start(f32[1,64]{1,0:T(1,128)S(1)} %get-tuple-element.71), channel_id=1, source_target_pairs={{0,1},{1,0},{2,3},{3,2},{4,5},{5,4},{6,7},{7,6},{8,9},{9,8},{10,11... | collective-permute-start | bytes 776 | tf_op jit(solution)/shard_map/ppermute | solution.py:40
  98.6 3.4 %collective-permute-start.16 = (f32[1,64]{1,0:T(1,128)S(1)}, f32[1,64]{1,0:T(1,128)S(1)}, u32[]{:S(2)}, u32[]{:S(2)}) collective-permute-start(f32[1,64]{1,0:T(1,128)S(1)} %add.12), channel_id=1, source_target_pairs={{0,2},{1,3},{2,0},{3,1},{4,6},{5,7},{6,4},{7,5},{8,10},{9,11},{10,... | collective-permute-start | bytes 776 | tf_op jit(solution)/shard_map/ppermute | solution.py:40
  101.9 2.1 %collective-permute-done.16 = f32[1,64]{1,0:T(1,128)S(1)} collective-permute-done((f32[1,64]{1,0:T(1,128)S(1)}, f32[1,64]{1,0:T(1,128)S(1)}, u32[]{:S(2)}, u32[]{:S(2)}) %collective-permute-start.16) | collective-permute-done | bytes 288 | tf_op jit(solution)/shard_map/ppermute | solution.py:40
  104.0 5.1 %collective-permute-start.17 = (f32[1,64]{1,0:T(1,128)S(1)}, f32[1,64]{1,0:T(1,128)S(1)}, u32[]{:S(2)}, u32[]{:S(2)}) collective-permute-start(f32[1,64]{1,0:T(1,128)S(1)} %add.13), channel_id=1, source_target_pairs={{0,4},{1,5},{2,6},{3,7},{4,0},{5,1},{6,2},{7,3},{8,12},{9,13},{10,... | collective-permute-start | bytes 776 | tf_op jit(solution)/shard_map/ppermute | solution.py:40
  110.7 4.4 %collective-permute-start.18 = (f32[1,64]{1,0:T(1,128)S(1)}, f32[1,64]{1,0:T(1,128)S(1)}, u32[]{:S(2)}, u32[]{:S(2)}) collective-permute-start(f32[1,64]{1,0:T(1,128)S(1)} %add.14), channel_id=1, source_target_pairs={{0,8},{1,9},{2,10},{3,11},{4,12},{5,13},{6,14},{7,15},{8,0},{9,1},... | collective-permute-start | bytes 776 | tf_op jit(solution)/shard_map/ppermute | solution.py:40
  115.0 2.0 %collective-permute-done.18 = f32[1,64]{1,0:T(1,128)S(1)} collective-permute-done((f32[1,64]{1,0:T(1,128)S(1)}, f32[1,64]{1,0:T(1,128)S(1)}, u32[]{:S(2)}, u32[]{:S(2)}) %collective-permute-start.18) | collective-permute-done | bytes 288 | tf_op jit(solution)/shard_map/ppermute | solution.py:40
  120.4 3.1 %collective-permute-done.9.north = f32[64,128]{1,0:T(8,128)S(1)} collective-permute-done((f32[64,128]{1,0:T(8,128)S(1)}, f32[64,128]{1,0:T(8,128)S(1)}, u32[]{:S(2)}, u32[]{:S(2)}) %collective-permute-start.9) | collective-permute-done | bytes 32800 | tf_op jit(solution)/shard_map/ppermute | solution.py:26
  123.5 3.9 %collective-permute-start.6 = (f32[64,256]{1,0:T(8,128)S(1)}, f32[64,256]{1,0:T(8,128)S(1)}, u32[]{:S(2)}, u32[]{:S(2)}) collective-permute-start(f32[64,256]{1,0:T(8,128)S(1)} %get-tuple-element.52), channel_id=1, source_target_pairs={{0,4},{4,8},{8,12},{1,5},{5,9},{9,13},{2,6},{6,10},{10,14},{3,7},{... | collective-permute-start | bytes 196616 | tf_op jit(solution)/shard_map/ppermute | solution.py:26
  127.4 1.9 %collective-permute-done.6.west = f32[64,256]{1,0:T(8,128)S(1)} collective-permute-done((f32[64,256]{1,0:T(8,128)S(1)}, f32[64,256]{1,0:T(8,128)S(1)}, u32[]{:S(2)}, u32[]{:S(2)}) %collective-permute-start.6) | collective-permute-done | bytes 65568 | tf_op jit(solution)/shard_map/ppermute | solution.py:26
  130.6 5.2 %collective-permute-done.7.east = f32[64,256]{1,0:T(8,128)S(1)} collective-permute-done((f32[64,256]{1,0:T(8,128)S(1)}, f32[64,256]{1,0:T(8,128)S(1)}, u32[]{:S(2)}, u32[]{:S(2)}) %collective-permute-start.7) | collective-permute-done | bytes 65568 | tf_op jit(solution)/shard_map/ppermute | solution.py:26
  137.2 3.1 %load.1.window = f32[27,4,64,256]{3,2,1,0:T(8,128)S(1)} custom-call(f32[64,7,64,256]{3,2,1,0:T(8,128)} %get-tuple-element.46.pack), custom_call_target="tpu_custom_call" | custom-call | flops 10485760 | bytes 4194304 | tf_op jit(solution)/shard_map/load/pallas_call | solution.py:767
  141.6 4.9 %shard_map.122 = (f32[64,64,256]{2,1,0:T(8,128)}, f32[18,4,64,256]{3,2,1,0:T(8,128)S(1)}, f32[4,64,256]{2,1,0:T(8,128)S(1)}) custom-call(f32[64]{0:T(128)S(1)} %copy-done.8, f32[64]{0:T(128)S(1)} %copy-done.9, f32[64]{0:T(128)S(1)} %copy-done.7, f32[64,7,64,256]{3,2,1,0:T(8,128)} %get-tuple-element.46.pack, f32[27,4,64,256]{3,2,1,0:T(8,128)S(1)} %load.1.window, ...), custom_call_target="tpu_custom_call" | custom-call | flops 36700160 | bytes 12845056 | tf_op jit(solution)/shard_map/pallas_call | solution.py:813
  146.5 3.5 %shard_map.123 = (f32[64,64,256]{2,1,0:T(8,128)}, f32[14,4,64,256]{3,2,1,0:T(8,128)S(1)}, f32[4,64,256]{2,1,0:T(8,128)S(1)}) custom-call(f32[64]{0:T(128)S(1)} %copy-done.8, f32[64]{0:T(128)S(1)} %copy-done.9, f32[64]{0:T(128)S(1)} %copy-done.7, f32[64,7,64,256]{3,2,1,0:T(8,128)} %get-tuple-element.46.pack, ...), custom_call_target="tpu_custom_call", output_to_operand_aliasing={{0}: (14, {})} | custom-call | flops 20971520 | bytes 7340032 | tf_op jit(solution)/shard_map/pallas_call | solution.py:813
  150.1 2.9 %shard_map.124 = (f32[64,64,256]{2,1,0:T(8,128)}, f32[8,4,64,256]{3,2,1,0:T(8,128)S(1)}, f32[4,64,256]{2,1,0:T(8,128)S(1)}) custom-call(f32[64]{0:T(128)S(1)} %copy-done.8, f32[64]{0:T(128)S(1)} %copy-done.9, f32[64]{0:T(128)S(1)} %copy-done.7, f32[64,7,64,256]{3,2,1,0:T(8,128)} %get-tuple-element.46.pack, ...), custom_call_target="tpu_custom_call", output_to_operand_aliasing={{0}: (14, {})} | custom-call | flops 15728640 | bytes 5505024 | tf_op jit(solution)/shard_map/pallas_call | solution.py:813
  153.0 2.1 %shard_map.125 = (f32[64,64,256]{2,1,0:T(8,128)}, f32[5,4,64,256]{3,2,1,0:T(8,128)S(1)}, f32[4,64,256]{2,1,0:T(8,128)S(1)}) custom-call(f32[64]{0:T(128)S(1)} %copy-done.8, f32[64]{0:T(128)S(1)} %copy-done.9, f32[64]{0:T(128)S(1)} %copy-done.7, f32[64,7,64,256]{3,2,1,0:T(8,128)} %get-tuple-element.46.pack, ...), custom_call_target="tpu_custom_call", output_to_operand_aliasing={{0}: (14, {})} | custom-call | flops 7864320 | bytes 2752512 | tf_op jit(solution)/shard_map/pallas_call | solution.py:813
  155.1 2.3 %shard_map.126 = (f32[64,64,256]{2,1,0:T(8,128)}, f32[1,64]{1,0:T(1,128)}) custom-call(f32[64]{0:T(128)S(1)} %copy-done.8, f32[64]{0:T(128)S(1)} %copy-done.9, f32[64]{0:T(128)S(1)} %copy-done.7, f32[64,7,64,256]{3,2,1,0:T(8,128)} %get-tuple-element.46.pack, f32[5,4,64,256]{3,2,1,0:T(8,128)S(1)} %get-tuple-element.69.window, ...), custom_call_target="tpu_custom_call", output_to_operand_aliasing={{0}: (16, {})} | custom-call | flops 2621440 | bytes 917504 | tf_op jit(solution)/shard_map/pallas_call | solution.py:813
  (60 shorter events, 22.9 us)
Async XLA Ops:
  3.4 136.9 %collective-permute-start.10 = (f32[28,64,256]{2,1,0:T(8,128)S(1)}, f32[28,64,256]{2,1,0:T(8,128)S(1)}, u32[]{:S(2)}, u32[]{:S(2)}) collective-permute-start(f32[28,64,256]{2,1,0:T(8,128)S(1)} %head.1), channel_id=1, source_target_pairs={{0,16},{1,17},{2,18},{3,19},{4,20},{5,21},{6,22},{7,23},{8,24},{9,... | collective-permute-start | bytes 5505032 | tf_op jit(solution)/shard_map/ppermute | solution.py:26
  17.7 11.4 %collective-permute-start = (f32[64,256]{1,0:T(8,128)}, f32[64,256]{1,0:T(8,128)S(1)}, u32[]{:S(2)}, u32[]{:S(2)}) collective-permute-start(f32[64,256]{1,0:T(8,128)} %get-tuple-element.39), channel_id=1, source_target_pairs={{0,4},{4,8},{8,12},{1,5},{5,9},{9,13},{2,6},{6,10},{10,14},{3,7},{... | collective-permute-start | bytes 196616 | tf_op jit(solution)/shard_map/ppermute | solution.py:26
  22.0 7.1 %collective-permute-start.1 = (f32[64,256]{1,0:T(8,128)}, f32[64,256]{1,0:T(8,128)S(1)}, u32[]{:S(2)}, u32[]{:S(2)}) collective-permute-start(f32[64,256]{1,0:T(8,128)} %get-tuple-element.40), channel_id=1, source_target_pairs={{4,0},{8,4},{12,8},{5,1},{9,5},{13,9},{6,2},{10,6},{14,10},{7,3},{... | collective-permute-start | bytes 196616 | tf_op jit(solution)/shard_map/ppermute | solution.py:26
  23.3 2.6 %collective-permute-start.2 = (f32[64,128]{1,0:T(8,128)}, f32[64,128]{1,0:T(8,128)S(1)}, u32[]{:S(2)}, u32[]{:S(2)}) collective-permute-start(f32[64,128]{1,0:T(8,128)} %get-tuple-element.41), channel_id=1, source_target_pairs={{0,1},{1,2},{2,3},{4,5},{5,6},{6,7},{8,9},{9,10},{10,11},{12,13},{... | collective-permute-start | bytes 98312 | tf_op jit(solution)/shard_map/ppermute | solution.py:26
  24.6 4.5 %collective-permute-start.3 = (f32[64,128]{1,0:T(8,128)}, f32[64,128]{1,0:T(8,128)S(1)}, u32[]{:S(2)}, u32[]{:S(2)}) collective-permute-start(f32[64,128]{1,0:T(8,128)} %get-tuple-element.42), channel_id=1, source_target_pairs={{1,0},{2,1},{3,2},{5,4},{6,5},{7,6},{9,8},{10,9},{11,10},{13,12},{... | collective-permute-start | bytes 98312 | tf_op jit(solution)/shard_map/ppermute | solution.py:26
  29.7 61.6 %copy-start.3 = (f32[192,256]{1,0:T(8,128)S(1)}, f32[192,256]{1,0:T(8,128)}, u32[]{:S(2)}) copy-start(f32[192,256]{1,0:T(8,128)} %get-tuple-element.49.edge_rate) | copy-start | bytes 589828
  29.7 61.6 %copy-start.5 = (f32[64,256]{1,0:T(8,128)S(1)}, f32[64,256]{1,0:T(8,128)}, u32[]{:S(2)}) copy-start(f32[64,256]{1,0:T(8,128)} %get-tuple-element.50.cu0) | copy-start | bytes 196612
  29.7 61.6 %copy-start.6 = (f32[64,128]{1,0:T(8,128)S(1)}, f32[64,128]{1,0:T(8,128)}, u32[]{:S(2)}) copy-start(f32[64,128]{1,0:T(8,128)} %get-tuple-element.51.cv0) | copy-start | bytes 98308
  29.7 61.6 %copy-start.7 = (f32[64]{0:T(128)S(1)}, f32[64]{0:T(128)}, u32[]{:S(2)}) copy-start(f32[64]{0:T(128)} %profile_hbm.11) | copy-start | bytes 772
  46.7 99.8 %collective-permute-start.11 = (f32[16,64,256]{2,1,0:T(8,128)}, f32[16,64,256]{2,1,0:T(8,128)S(1)}, u32[]{:S(2)}, u32[]{:S(2)}) collective-permute-start(f32[16,64,256]{2,1,0:T(8,128)} %get-tuple-element.58), channel_id=1, source_target_pairs={{0,16},{1,17},{2,18},{3,19},{4,20},{5,21},{6,22},{7,23},{8,24},{9,... | collective-permute-start | bytes 3145736 | tf_op jit(solution)/shard_map/ppermute | solution.py:26
  48.1 102.0 %collective-permute-start.12 = (f32[12,64,256]{2,1,0:T(8,128)}, f32[12,64,256]{2,1,0:T(8,128)S(1)}, u32[]{:S(2)}, u32[]{:S(2)}) collective-permute-start(f32[12,64,256]{2,1,0:T(8,128)} %get-tuple-element.62), channel_id=1, source_target_pairs={{0,16},{1,17},{2,18},{3,19},{4,20},{5,21},{6,22},{7,23},{8,24},{9,... | collective-permute-start | bytes 2359304 | tf_op jit(solution)/shard_map/ppermute | solution.py:26
  49.4 41.8 %collective-permute-start.4 = (f32[192,256]{1,0:T(8,128)}, f32[192,256]{1,0:T(8,128)S(1)}, u32[]{:S(2)}, u32[]{:S(2)}) collective-permute-start(f32[192,256]{1,0:T(8,128)} %get-tuple-element.47.mine), channel_id=1, source_target_pairs={{0,16},{1,17},{2,18},{3,19},{4,20},{5,21},{6,22},{7,23},{8,24},{9,... | collective-permute-start | bytes 589832 | tf_op jit(solution)/shard_map/ppermute | solution.py:26
  50.7 6.4 %collective-permute-start.5 = (f32[64,256]{1,0:T(8,128)}, f32[64,256]{1,0:T(8,128)S(1)}, u32[]{:S(2)}, u32[]{:S(2)}) collective-permute-start(f32[64,256]{1,0:T(8,128)} %get-tuple-element.48), channel_id=1, source_target_pairs={{16,0},{17,1},{18,2},{19,3},{20,4},{21,5},{22,6},{23,7},{24,8},{25... | collective-permute-start | bytes 196616 | tf_op jit(solution)/shard_map/ppermute | solution.py:26
  57.1 95.9 %collective-permute-start.13 = (f32[6,64,256]{2,1,0:T(8,128)}, f32[6,64,256]{2,1,0:T(8,128)S(1)}, u32[]{:S(2)}, u32[]{:S(2)}) collective-permute-start(f32[6,64,256]{2,1,0:T(8,128)} %get-tuple-element.66), channel_id=1, source_target_pairs={{0,16},{1,17},{2,18},{3,19},{4,20},{5,21},{6,22},{7,23},{8,24},{9,... | collective-permute-start | bytes 1179656 | tf_op jit(solution)/shard_map/ppermute | solution.py:26
  92.4 6.1 %collective-permute-start.15 = (f32[1,64]{1,0:T(1,128)S(1)}, f32[1,64]{1,0:T(1,128)S(1)}, u32[]{:S(2)}, u32[]{:S(2)}) collective-permute-start(f32[1,64]{1,0:T(1,128)S(1)} %get-tuple-element.71), channel_id=1, source_target_pairs={{0,1},{1,0},{2,3},{3,2},{4,5},{5,4},{6,7},{7,6},{8,9},{9,8},{10,11... | collective-permute-start | bytes 776 | tf_op jit(solution)/shard_map/ppermute | solution.py:40
  98.6 5.5 %collective-permute-start.16 = (f32[1,64]{1,0:T(1,128)S(1)}, f32[1,64]{1,0:T(1,128)S(1)}, u32[]{:S(2)}, u32[]{:S(2)}) collective-permute-start(f32[1,64]{1,0:T(1,128)S(1)} %add.12), channel_id=1, source_target_pairs={{0,2},{1,3},{2,0},{3,1},{4,6},{5,7},{6,4},{7,5},{8,10},{9,11},{10,... | collective-permute-start | bytes 776 | tf_op jit(solution)/shard_map/ppermute | solution.py:40
  104.0 6.6 %collective-permute-start.17 = (f32[1,64]{1,0:T(1,128)S(1)}, f32[1,64]{1,0:T(1,128)S(1)}, u32[]{:S(2)}, u32[]{:S(2)}) collective-permute-start(f32[1,64]{1,0:T(1,128)S(1)} %add.13), channel_id=1, source_target_pairs={{0,4},{1,5},{2,6},{3,7},{4,0},{5,1},{6,2},{7,3},{8,12},{9,13},{10,... | collective-permute-start | bytes 776 | tf_op jit(solution)/shard_map/ppermute | solution.py:40
  110.7 6.3 %collective-permute-start.18 = (f32[1,64]{1,0:T(1,128)S(1)}, f32[1,64]{1,0:T(1,128)S(1)}, u32[]{:S(2)}, u32[]{:S(2)}) collective-permute-start(f32[1,64]{1,0:T(1,128)S(1)} %add.14), channel_id=1, source_target_pairs={{0,8},{1,9},{2,10},{3,11},{4,12},{5,13},{6,14},{7,15},{8,0},{9,1},... | collective-permute-start | bytes 776 | tf_op jit(solution)/shard_map/ppermute | solution.py:40
  117.0 2.1 %collective-permute-start.8 = (f32[64,128]{1,0:T(8,128)S(1)}, f32[64,128]{1,0:T(8,128)S(1)}, u32[]{:S(2)}, u32[]{:S(2)}) collective-permute-start(f32[64,128]{1,0:T(8,128)S(1)} %get-tuple-element.54), channel_id=1, source_target_pairs={{0,1},{1,2},{2,3},{4,5},{5,6},{6,7},{8,9},{9,10},{10,11},{12,13},{... | collective-permute-start | bytes 98312 | tf_op jit(solution)/shard_map/ppermute | solution.py:26
  119.1 4.4 %collective-permute-start.9 = (f32[64,128]{1,0:T(8,128)S(1)}, f32[64,128]{1,0:T(8,128)S(1)}, u32[]{:S(2)}, u32[]{:S(2)}) collective-permute-start(f32[64,128]{1,0:T(8,128)S(1)} %get-tuple-element.55), channel_id=1, source_target_pairs={{1,0},{2,1},{3,2},{5,4},{6,5},{7,6},{9,8},{10,9},{11,10},{13,12},{... | collective-permute-start | bytes 98312 | tf_op jit(solution)/shard_map/ppermute | solution.py:26
  123.5 5.8 %collective-permute-start.6 = (f32[64,256]{1,0:T(8,128)S(1)}, f32[64,256]{1,0:T(8,128)S(1)}, u32[]{:S(2)}, u32[]{:S(2)}) collective-permute-start(f32[64,256]{1,0:T(8,128)S(1)} %get-tuple-element.52), channel_id=1, source_target_pairs={{0,4},{4,8},{8,12},{1,5},{5,9},{9,13},{2,6},{6,10},{10,14},{3,7},{... | collective-permute-start | bytes 196616 | tf_op jit(solution)/shard_map/ppermute | solution.py:26
  129.3 6.5 %collective-permute-start.7 = (f32[64,256]{1,0:T(8,128)S(1)}, f32[64,256]{1,0:T(8,128)S(1)}, u32[]{:S(2)}, u32[]{:S(2)}) collective-permute-start(f32[64,256]{1,0:T(8,128)S(1)} %get-tuple-element.53), channel_id=1, source_target_pairs={{4,0},{8,4},{12,8},{5,1},{9,5},{13,9},{6,2},{10,6},{14,10},{7,3},{... | collective-permute-start | bytes 196616 | tf_op jit(solution)/shard_map/ppermute | solution.py:26
  135.8 19.3 %collective-permute-start.14 = (f32[2,64,256]{2,1,0:T(8,128)}, f32[2,64,256]{2,1,0:T(8,128)S(1)}, u32[]{:S(2)}, u32[]{:S(2)}) collective-permute-start(f32[2,64,256]{2,1,0:T(8,128)} %get-tuple-element.70), channel_id=1, source_target_pairs={{0,16},{1,17},{2,18},{3,19},{4,20},{5,21},{6,22},{7,23},{8,24},{9,... | collective-permute-start | bytes 393224 | tf_op jit(solution)/shard_map/ppermute | solution.py:26
  140.3 14.9 %collective-permute-start.19 = (f32[1,64]{1,0:T(1,128)S(1)}, f32[1,64]{1,0:T(1,128)S(1)}, u32[]{:S(2)}, u32[]{:S(2)}) collective-permute-start(f32[1,64]{1,0:T(1,128)S(1)} %add.15.rest_0_), channel_id=1, source_target_pairs={{0,16},{1,17},{2,18},{3,19},{4,20},{5,21},{6,22},{7,23},{8,24},{9,... | collective-permute-start | bytes 776 | tf_op jit(solution)/shard_map/ppermute | solution.py:26
  (11 other events, 86.0 us)

commit v2 on v1

--- a/solution.py
+++ b/solution.py
@@ -129,8 +129,13 @@
 
 def here_of(cells, v, dims):
     _, rows, cols, grid_y = dims
-    x = cells[v] // grid_y - lax.axis_index("gx") * rows
-    y = lax.rem(cells[v], grid_y) - lax.axis_index("gy") * cols
+    cell = cells[v]
+    if grid_y & (grid_y - 1):
+        line = cell // grid_y
+    else:
+        line = lax.shift_right_logical(cell, jnp.int32(grid_y.bit_length() - 1))
+    x = line - lax.axis_index("gx") * rows
+    y = cell - line * grid_y - lax.axis_index("gy") * cols
     return x, y, (x >= 0) & (x < rows) & (y >= 0) & (y < cols)
 
 
@@ -151,14 +156,28 @@
                 block = source[z, pl.ds(top, SUBLANES), pl.ds(base, LANES)]
                 got = jnp.where(lane == z, lane_to(block, low, z), got)
             got = pltpu.roll(got, lax.rem(SUBLANES - lax.rem(x, SUBLANES), SUBLANES), 0)[0:1]
-            put_row(target, 2 * levels + v, got, slice(LANES, 2 * LANES))
+            put_row(target, v, got, slice(0, LANES))
 
         return carry
 
     lax.fori_loop(0, cells.shape[0], one, 0)
 
 
-def gather_edges(source, target, dims):
+def put_columns(target, columns, dims):
+    levels, rows = dims[:2]
+    half = rows // 2
+    at = slice(2 * levels, 2 * levels + half)
+    target[at, 0:LANES] = columns[0:half]
+    target[at, LANES : 2 * LANES] = columns[half:rows]
+
+
+def get_columns(source, dims):
+    levels, rows = dims[:2]
+    at = slice(2 * levels, 2 * levels + rows // 2)
+    return jnp.concatenate([source[at, 0:LANES], source[at, LANES : 2 * LANES]], axis=0)
+
+
+def gather_edges(source, target, dims, blocks=1, ready=lambda b: None):
     levels, rows, cols, _ = dims
     _, lane = iotas(rows, LANES)
 
@@ -179,8 +198,12 @@
         return columns
 
     zero = jnp.zeros((rows, LANES), jnp.float32)
-    columns = lax.fori_loop(0, levels // SUBLANES, group, zero)
-    target[2 * levels : 2 * levels + rows, 0:LANES] = columns
+    columns = zero
+    groups = levels // SUBLANES // blocks
+    for b in range(blocks):
+        ready(b)
+        columns = lax.fori_loop(b * groups, (b + 1) * groups, group, columns)
+    put_columns(target, columns, dims)
 
 
 def head_kernel(slot_hbm, fields, out, slot, sems):
@@ -214,6 +237,8 @@
     out_column,
     out_edges,
     out_edge_rate,
+    out_vents,
+    out_vent_rate,
     slot,
     horiz,
     class_rates,
@@ -229,8 +254,8 @@
     adj = lax.axis_index("section")
     flag = adj.astype(jnp.float32)
     courants = [
-        pltpu.make_async_copy(cv_hbm.at[:, :, pl.ds(0, LANES)], cv, sems.at[1]),
-        pltpu.make_async_copy(cu_hbm.at[:, pl.ds(0, SUBLANES), :], cu, sems.at[2]),
+        pltpu.make_async_copy(cv_hbm.at[:, :, pl.ds(0, LANES)], cv, sems.at[0]),
+        pltpu.make_async_copy(cu_hbm.at[:, pl.ds(0, SUBLANES), :], cu, sems.at[1]),
     ]
     small = [
         pltpu.make_async_copy(a, b, small_sems.at[i])
@@ -246,9 +271,21 @@
     ]
     for copy in small:
         copy.start()
+    for copy in courants:
+        copy.start()
     for copy in small:
         copy.wait()
-    copies = [pltpu.make_async_copy(fields.at[0, slot[adj]], field, sems.at[0])] + courants
+    blocks = sems.shape[0] - 2
+    size = levels // blocks
+    pick = slot[adj]
+    copies = [
+        pltpu.make_async_copy(
+            fields.at[0, pick, pl.ds(b * size, size)],
+            field.at[pl.ds(b * size, size)],
+            sems.at[2 + b],
+        )
+        for b in range(blocks)
+    ]
     for copy in copies:
         copy.start()
 
@@ -258,10 +295,8 @@
         rate = jnp.where(kinds == kind, class_rates[kind], rate)
     out_rate[...] = rate
     out_column[...] = jnp.zeros((rows, cols), jnp.float32)
-    tail = slice(2 * levels, out_edges.shape[0])
-    blank = jnp.zeros((out_edges.shape[0] - 2 * levels, cols), jnp.float32)
-    out_edges[tail, :] = blank
-    out_edge_rate[tail, :] = blank
+    out_vents[...] = jnp.zeros(out_vents.shape, jnp.float32)
+    out_vent_rate[...] = jnp.zeros(out_vent_rate.shape, jnp.float32)
     _, line_col = iotas(1, cols)
 
     def one(v, carry):
@@ -274,7 +309,7 @@
             put_row(out_column, x, line)
             found = jnp.sum(jnp.where(hit, get_row(out_rate, x), 0.0), axis=1, keepdims=True)
             found = jnp.broadcast_to(found, (1, LANES))
-            put_row(out_edge_rate, 2 * levels + v, found, slice(LANES, 2 * LANES))
+            put_row(out_vent_rate, v, found)
 
         return carry
 
@@ -282,15 +317,12 @@
     out_edge_rate[0:levels, :] = jnp.broadcast_to(rate[0:1, :], (levels, cols))
     out_edge_rate[levels : 2 * levels, :] = jnp.broadcast_to(rate[rows - 1 : rows, :], (levels, cols))
     _, lane = iotas(rows, LANES)
-    out_edge_rate[2 * levels : 2 * levels + rows, 0:LANES] = jnp.where(
-        lane < levels, rate[:, 0:1], rate[:, cols - 1 : cols]
+    put_columns(
+        out_edge_rate, jnp.where(lane < levels, rate[:, 0:1], rate[:, cols - 1 : cols]), dims
     )
 
-    copies[0].wait()
-    gather_edges(field, out_edges, dims)
-    gather_vents(cells, field, out_edges, dims)
-    copies[1].wait()
-    copies[2].wait()
+    for copy in courants:
+        copy.wait()
 
     def group(i, columns):
         base = pl.multiple_of(i * SUBLANES, SUBLANES)
@@ -306,7 +338,9 @@
 
     zero = jnp.zeros((rows, LANES), jnp.float32)
     out_cv0[...] = lax.fori_loop(0, levels // SUBLANES, group, zero)
-    columns = out_edges[2 * levels : 2 * levels + rows, 0:LANES]
+    gather_edges(field, out_edges, dims, blocks, lambda b: copies[b].wait())
+    gather_vents(cells, field, out_vents, dims)
+    columns = get_columns(out_edges, dims)
     out_xf[...] = out_edges[levels : 2 * levels, :]
     out_xb[...] = out_cu0[...] * out_edges[0:levels, :]
     out_yf[...] = pltpu.roll(columns, LANES - levels, 1)
@@ -339,10 +373,10 @@
     north,
     rate,
     column,
-    edges,
+    vents,
     *rest,
 ):
-    levels, _, cols, _ = dims
+    levels, _, _, _ = dims
     out_pack, out_edges, out_vents = rest[:3]
     out_chunks = rest[3 : 3 + len(chunks)]
     slot, horiz, vert, profile, cells = rest[3 + len(chunks) : 8 + len(chunks)]
@@ -377,8 +411,8 @@
             for other in loads[b]:
                 other.start()
         loads[b].append(copy)
-    tail = slice(2 * levels, out_edges.shape[0])
-    out_edges[tail, :] = jnp.zeros((out_edges.shape[0] - 2 * levels, cols), jnp.float32)
+    out_vents[:, 0:LANES] = jnp.zeros(vents.shape, jnp.float32)
+    out_vents[:, LANES : 2 * LANES] = vents[...]
     sides = Sides(west, east, south, north)
 
     def planes(adjoint, low, high):
@@ -424,10 +458,7 @@
         store.start()
         stores.append(store)
     gather_edges(first, out_edges, dims)
-    gather_vents(cells, first, out_edges, dims)
-    at = slice(2 * levels, 2 * levels + out_vents.shape[0])
-    out_vents[:, 0:LANES] = out_edges[at, LANES : 2 * LANES]
-    out_vents[:, LANES : 2 * LANES] = edges[at, LANES : 2 * LANES]
+    gather_vents(cells, first, out_vents, dims)
     for store in stores:
         store.wait()
 
@@ -437,9 +468,11 @@
     profile,
     mine,
     theirs,
+    my_vents,
     at_vents,
     edges,
     edge_rate,
+    vent_rate,
     cu0,
     cv0,
     out_rim,
@@ -449,21 +482,19 @@
     out_yb,
     out_terms,
 ):
-    levels, rows, _, _ = dims
+    levels, _, _, _ = dims
     adj = lax.axis_index("section")
     lam = mine[...] - edge_rate[...] * slope(theirs[...]) * edges[...]
     rim = jnp.where(adj == 1, lam, mine[...])
     out_rim[...] = rim
-    columns = rim[2 * levels : 2 * levels + rows, 0:LANES]
+    columns = get_columns(rim, dims)
     out_xf[...] = rim[levels : 2 * levels, :]
     out_xb[...] = cu0[...] * rim[0:levels, :]
     out_yf[...] = pltpu.roll(columns, LANES - levels, 1)
     out_yb[...] = cv0[...] * columns
     vents = out_terms.shape[1]
-    at = slice(2 * levels, 2 * levels + vents)
-    right = slice(LANES, 2 * LANES)
-    lam_two = at_vents[:, right]
-    loss = edge_rate[at, right] * slope(mine[at, right]) * lam_two
+    lam_two = at_vents[:, LANES : 2 * LANES]
+    loss = vent_rate[...] * slope(my_vents[:, 0:LANES]) * lam_two
     both = at_vents[:, 0:LANES] - loss + lam_two
     weights = jnp.concatenate(
         [profile[...], jnp.zeros((1, LANES - levels), jnp.float32)], axis=1
@@ -569,7 +600,7 @@
             value = value - rate[...] * wash(here) + profile[z] * column[...]
             value = window[j, 0] - rate[...] * slope(value) * window[j, 3]
             row, col = iotas(rows, cols)
-            columns = rim[2 * levels : 2 * levels + rows, 0:LANES]
+            columns = get_columns(rim, dims)
             value = jnp.where(col == 0, wide(lane_to(columns, z, 0), cols), value)
             value = jnp.where(
                 col == cols - 1, wide(lane_to(columns, z + levels, LANES - 1), cols), value
@@ -628,7 +659,7 @@
 
 
 def cuts(levels):
-    sizes = [levels * part // 64 for part in (28, 16, 12, 6)]
+    sizes = [levels * part // 64 for part in (32, 16, 10, 4)]
     sizes.append(levels - sum(sizes))
     bounds = [0]
     for size in sizes:
@@ -654,7 +685,7 @@
     grid_y = cols * lax.axis_size("gy")
     dims = (levels, rows, cols, grid_y)
     cells = levels * rows * cols
-    edge_rows = 2 * levels + max(rows, vents)
+    edge_rows = 2 * levels + rows // 2
     f32 = jnp.float32
     i32 = jnp.int32
     shape = jax.ShapeDtypeStruct
@@ -663,6 +694,7 @@
     side = shape((rows, LANES), f32)
     flat = shape((rows, cols), f32)
     rims = shape((edge_rows, cols), f32)
+    vent_rows = shape((vents, LANES), f32)
     pieces = cuts(levels)
 
     whole_vmem = pltpu.CompilerParams(vmem_limit_bytes=58 * 1024 * 1024)
@@ -685,12 +717,15 @@
     )(slot_pick, fields)
     received = [send(start)]
 
-    xf, xb, yf, yb, cu0, cv0, rate, column, edges, edge_rate = pl.pallas_call(
+    (
+        xf, xb, yf, yb, cu0, cv0, rate, column, edges, edge_rate, my_vents, vent_rates
+    ) = pl.pallas_call(
         functools.partial(edges_kernel, dims),
         name="edges",
         in_specs=[hbm()] * 8 + [vmem()],
-        out_specs=[vmem()] * 10,
-        out_shape=[line, line, side, side, line, side, flat, flat, rims, rims],
+        out_specs=[vmem()] * 12,
+        out_shape=[line, line, side, side, line, side, flat, flat, rims, rims]
+        + [vent_rows] * 2,
         scratch_shapes=[
             pltpu.SMEM(slot_pick.shape, i32),
             pltpu.SMEM(horiz_diff.shape, f32),
@@ -701,7 +736,7 @@
             pltpu.VMEM((levels, SUBLANES, cols), f32),
             pltpu.VMEM((levels, rows, LANES), f32),
             pltpu.SemaphoreType.DMA((5,)),
-            pltpu.SemaphoreType.DMA((3,)),
+            pltpu.SemaphoreType.DMA((6,)),
         ],
         compiler_params=whole_vmem,
         cost_estimate=cost(cells, 10, 2),
@@ -716,8 +751,8 @@
     north = neighbour(yb, "gy", -1)
 
     levels_smem = [pltpu.SMEM((levels,), f32)] * 3
-    blocks = 4
-    pack, mine, at_vents, *later = pl.pallas_call(
+    blocks = 8
+    pack, mine, my_vents, *later = pl.pallas_call(
         functools.partial(first_kernel, dims, pieces[1:], blocks),
         name="first",
         in_specs=[hbm()] * 8 + [vmem()] * 7,
@@ -738,23 +773,25 @@
         cost_estimate=cost(cells, 40, 5),
     )(
         slot_pick, horiz_diff, vert_diff, profile, vent_cells,
-        fields, courant_x, courant_y, west, east, south, north, rate, column, edges,
+        fields, courant_x, courant_y, west, east, south, north, rate, column, my_vents,
     )
 
     theirs = send(mine)
-    at_vents = neighbour(at_vents, "section", -1)
+    at_vents = neighbour(my_vents, "section", -1)
     for piece in later:
         received.append(send(piece))
 
     rim, xf, xb, yf, yb, terms = pl.pallas_call(
         functools.partial(rim_kernel, dims),
         name="rim",
-        in_specs=[vmem()] * 8,
+        in_specs=[vmem()] * 10,
         out_specs=[vmem()] * 6,
         out_shape=[rims, line, line, side, side, shape((1, vents), f32)],
         compiler_params=params,
         cost_estimate=cost(edge_rows * cols, 20, 5),
-    )(profile[None, :], mine, theirs, at_vents, edges, edge_rate, cu0, cv0)
+    )(
+        profile[None, :], mine, theirs, my_vents, at_vents, edges, edge_rate, vent_rates, cu0, cv0
+    )
     west = neighbour(xf, "gx", 1)
     east = neighbour(xb, "gx", -1)
     south = neighbour(yf, "gy", 1)
@@ -776,7 +813,7 @@
     )(pack)
 
     steps = doubling_steps()
-    while len(steps) > 2:
+    while len(steps) > 3:
         terms = terms + partner(terms, steps.pop(0))
 
     result = carry = None
@@ -787,7 +824,7 @@
         outs = out1 - out0
         if steps:
             more = partner(terms, steps.pop(0))
-        elif j == 2:
+        elif j == 3:
             passed = neighbour(terms, "section", 1)
         operands = [
             horiz_diff, vert_diff, profile, pack, window,
@@ -830,7 +867,7 @@
         )(*operands)
         if following:
             window, carry = state
-            if j < 2:
+            if j < 3:
                 terms = terms + more
         else:
             (terms,) = state

time: 159 us -> 154 us (0.969)
  starting transfers between devices: 48.7 us -> 43.2 us
    ppermute x4, starting transfers between devices: 18.2 us -> 13.3 us  [partner(): return lax.ppermute(value, ('section', 'gx', 'gy'), pairs)]
    ppermute x16, waiting for transfers between devices: 51.8 us -> 53.8 us  [neighbour(): return lax.ppermute(value, axis, pairs)]
  transfers between devices with their start and end apart: 20 -> 20, of which waited for: 11 -> 10; matrix products, arithmetic and copies ran while one was open for 0% -> 0% of each run, Pallas kernels for 27% -> 27%
where the time goes in v2:
time: 154 us; the launch traced here: 153 us
  waiting for transfers between devices  59.5 us (39%)
  Pallas kernels  46.1 us (30%)
  starting transfers between devices  43.2 us (28%)
  local copies, waits for them, and re-layouts  3.09 us (2%)
    ppermute x16, waiting for transfers between devices, neighbour(): return lax.ppermute(value, axis, pairs)  53.8 us
    ppermute x16, starting transfers between devices, neighbour(): return lax.ppermute(value, axis, pairs)  30 us
    pallas_call x1, Pallas kernels, program(): pl.pallas_call(functools.partial(first_kernel, dims, pieces[1:], blocks),...  16.2 us
    pallas_call x5, Pallas kernels, program(): pl.pallas_call(functools.partial(chunk_kernel, dims, piece, following), i...  15.8 us
    ppermute x4, starting transfers between devices, partner(): return lax.ppermute(value, ('section', 'gx', 'gy'), pairs)  13.3 us
    pallas_call x1, Pallas kernels, program(): pl.pallas_call(functools.partial(edges_kernel, dims), name='edges', in_sp...  8.47 us
    ppermute x4, waiting for transfers between devices, partner(): return lax.ppermute(value, ('section', 'gx', 'gy'), pairs)  5.71 us
    pallas_call x1, Pallas kernels, program(): pl.pallas_call(functools.partial(load_kernel, window_of(pieces[0], levels...  3.37 us
  transfers between devices with their start and end apart: 20, of which 10 were waited for; matrix products, arithmetic and copies ran while one was open for 0% of the time, Pallas kernels for 27%

profile of v2, /device:TPU:0, one launch (start us, length us, event | category | flops | bytes accessed | tf_op | source)
XLA Modules:
  0.0 153.0 jit_solution(17048241787837721674)
XLA Ops:
  1.3 2.2 %head.1 = f32[32,64,256]{2,1,0:T(8,128)S(1)} custom-call(s32[4]{0:T(128)S(1)} %copy-done.12, f32[1,4,64,64,256]{4,3,2,1,0:T(8,128)} %fields.5), custom_call_target="tpu_custom_call" | custom-call | flops 1048576 | bytes 4194304 | tf_op jit(solution)/shard_map/head/pallas_call | solution.py:708
  3.5 5.0 %collective-permute-start.10 = (f32[32,64,256]{2,1,0:T(8,128)S(1)}, f32[32,64,256]{2,1,0:T(8,128)S(1)}, u32[]{:S(2)}, u32[]{:S(2)}) collective-permute-start(f32[32,64,256]{2,1,0:T(8,128)S(1)} %head.1), channel_id=1, source_target_pairs={{0,16},{1,17},{2,18},{3,19},{4,20},{5,21},{6,22},{7,23},{8,24},{9,... | collective-permute-start | bytes 6291464 | tf_op jit(solution)/shard_map/ppermute | solution.py:26
  8.5 8.5 %edges.1 = (f32[64,256]{1,0:T(8,128)}, f32[64,256]{1,0:T(8,128)}, f32[64,128]{1,0:T(8,128)}, f32[64,128]{1,0:T(8,128)}, f32[64,256]{1,0:T(8,128)}, /*index=5*/f3...) custom-call(s32[4]{0:T(128)} %slot_hbm.5, ...), custom_call_target="tpu_custom_call" | custom-call | flops 10485760 | bytes 8388608 | tf_op jit(solution)/shard_map/edges/pallas_call | solution.py:722
  17.0 4.6 %collective-permute-start = (f32[64,256]{1,0:T(8,128)}, f32[64,256]{1,0:T(8,128)S(1)}, u32[]{:S(2)}, u32[]{:S(2)}) collective-permute-start(f32[64,256]{1,0:T(8,128)} %get-tuple-element.41), channel_id=1, source_target_pairs={{0,4},{4,8},{8,12},{1,5},{5,9},{9,13},{2,6},{6,10},{10,14},{3,7},{... | collective-permute-start | bytes 196616 | tf_op jit(solution)/shard_map/ppermute | solution.py:26
  25.5 2.9 %collective-permute-done.3.north = f32[64,128]{1,0:T(8,128)S(1)} collective-permute-done((f32[64,128]{1,0:T(8,128)}, f32[64,128]{1,0:T(8,128)S(1)}, u32[]{:S(2)}, u32[]{:S(2)}) %collective-permute-start.3) | collective-permute-done | bytes 32800 | tf_op jit(solution)/shard_map/ppermute | solution.py:26
  29.1 16.2 %first.1 = (f32[64,7,64,256]{3,2,1,0:T(8,128)}, f32[160,256]{1,0:T(8,128)}, f32[64,256]{1,0:T(8,128)}, f32[16,64,256]{2,1,0:T(8,128)}, f32[10,64,256]{2,1,0:T(8,...) custom-call(s32[4]{0:T(128)} %slot_hbm.5, f32[64]{0:T(128)} %horiz_hbm.13, f32[64]{0:T(128)} %vert_hbm.11, ...), custom_call_target="tpu_custom_call" | custom-call | flops 41943040 | bytes 20971520 | tf_op jit(solution)/shard_map/first/pallas_call | solution.py:755
  45.3 1.4 collective-permute-start.11
  50.6 5.1 %collective-permute-done.5.at_vents = f32[64,256]{1,0:T(8,128)S(1)} collective-permute-done((f32[64,256]{1,0:T(8,128)}, f32[64,256]{1,0:T(8,128)S(1)}, u32[]{:S(2)}, u32[]{:S(2)}) %collective-permute-start.5) | collective-permute-done | bytes 65568 | tf_op jit(solution)/shard_map/ppermute | solution.py:26
  55.6 37.7 %collective-permute-done.4.theirs = f32[160,256]{1,0:T(8,128)S(1)} collective-permute-done((f32[160,256]{1,0:T(8,128)}, f32[160,256]{1,0:T(8,128)S(1)}, u32[]{:S(2)}, u32[]{:S(2)}) %collective-permute-start.4) | collective-permute-done | bytes 163872 | tf_op jit(solution)/shard_map/ppermute | solution.py:26
  95.3 1.9 %collective-permute-start.15 = (f32[1,64]{1,0:T(1,128)S(1)}, f32[1,64]{1,0:T(1,128)S(1)}, u32[]{:S(2)}, u32[]{:S(2)}) collective-permute-start(f32[1,64]{1,0:T(1,128)S(1)} %get-tuple-element.75), channel_id=1, source_target_pairs={{0,1},{1,0},{2,3},{3,2},{4,5},{5,4},{6,7},{7,6},{8,9},{9,8},{10,11... | collective-permute-start | bytes 776 | tf_op jit(solution)/shard_map/ppermute | solution.py:40
  98.4 3.4 %collective-permute-start.16 = (f32[1,64]{1,0:T(1,128)S(1)}, f32[1,64]{1,0:T(1,128)S(1)}, u32[]{:S(2)}, u32[]{:S(2)}) collective-permute-start(f32[1,64]{1,0:T(1,128)S(1)} %add.12), channel_id=1, source_target_pairs={{0,2},{1,3},{2,0},{3,1},{4,6},{5,7},{6,4},{7,5},{8,10},{9,11},{10,... | collective-permute-start | bytes 776 | tf_op jit(solution)/shard_map/ppermute | solution.py:40
  101.8 2.1 %collective-permute-done.16 = f32[1,64]{1,0:T(1,128)S(1)} collective-permute-done((f32[1,64]{1,0:T(1,128)S(1)}, f32[1,64]{1,0:T(1,128)S(1)}, u32[]{:S(2)}, u32[]{:S(2)}) %collective-permute-start.16) | collective-permute-done | bytes 288 | tf_op jit(solution)/shard_map/ppermute | solution.py:40
  103.8 3.5 %collective-permute-start.17 = (f32[1,64]{1,0:T(1,128)S(1)}, f32[1,64]{1,0:T(1,128)S(1)}, u32[]{:S(2)}, u32[]{:S(2)}) collective-permute-start(f32[1,64]{1,0:T(1,128)S(1)} %add.13), channel_id=1, source_target_pairs={{0,4},{1,5},{2,6},{3,7},{4,0},{5,1},{6,2},{7,3},{8,12},{9,13},{10,... | collective-permute-start | bytes 776 | tf_op jit(solution)/shard_map/ppermute | solution.py:40
  109.3 4.5 %collective-permute-start.18 = (f32[1,64]{1,0:T(1,128)S(1)}, f32[1,64]{1,0:T(1,128)S(1)}, u32[]{:S(2)}, u32[]{:S(2)}) collective-permute-start(f32[1,64]{1,0:T(1,128)S(1)} %add.14), channel_id=1, source_target_pairs={{0,8},{1,9},{2,10},{3,11},{4,12},{5,13},{6,14},{7,15},{8,0},{9,1},... | collective-permute-start | bytes 776 | tf_op jit(solution)/shard_map/ppermute | solution.py:40
  113.8 1.9 %collective-permute-done.18 = f32[1,64]{1,0:T(1,128)S(1)} collective-permute-done((f32[1,64]{1,0:T(1,128)S(1)}, f32[1,64]{1,0:T(1,128)S(1)}, u32[]{:S(2)}, u32[]{:S(2)}) %collective-permute-start.18) | collective-permute-done | bytes 288 | tf_op jit(solution)/shard_map/ppermute | solution.py:40
  118.7 3.5 %collective-permute-start.6 = (f32[64,256]{1,0:T(8,128)S(1)}, f32[64,256]{1,0:T(8,128)S(1)}, u32[]{:S(2)}, u32[]{:S(2)}) collective-permute-start(f32[64,256]{1,0:T(8,128)S(1)} %get-tuple-element.56), channel_id=1, source_target_pairs={{0,4},{4,8},{8,12},{1,5},{5,9},{9,13},{2,6},{6,10},{10,14},{3,7},{... | collective-permute-start | bytes 196616 | tf_op jit(solution)/shard_map/ppermute | solution.py:26
  122.2 1.9 %collective-permute-done.6.west = f32[64,256]{1,0:T(8,128)S(1)} collective-permute-done((f32[64,256]{1,0:T(8,128)S(1)}, f32[64,256]{1,0:T(8,128)S(1)}, u32[]{:S(2)}, u32[]{:S(2)}) %collective-permute-start.6) | collective-permute-done | bytes 65568 | tf_op jit(solution)/shard_map/ppermute | solution.py:26
  125.4 5.7 %collective-permute-done.7.east = f32[64,256]{1,0:T(8,128)S(1)} collective-permute-done((f32[64,256]{1,0:T(8,128)S(1)}, f32[64,256]{1,0:T(8,128)S(1)}, u32[]{:S(2)}, u32[]{:S(2)}) %collective-permute-start.7) | collective-permute-done | bytes 65568 | tf_op jit(solution)/shard_map/ppermute | solution.py:26
  132.4 3.4 %load.1.window = f32[31,4,64,256]{3,2,1,0:T(8,128)S(1)} custom-call(f32[64,7,64,256]{3,2,1,0:T(8,128)} %get-tuple-element.48.pack), custom_call_target="tpu_custom_call" | custom-call | flops 10485760 | bytes 4194304 | tf_op jit(solution)/shard_map/load/pallas_call | solution.py:804
  137.1 5.5 %shard_map.122 = (f32[64,64,256]{2,1,0:T(8,128)}, f32[18,4,64,256]{3,2,1,0:T(8,128)S(1)}, f32[4,64,256]{2,1,0:T(8,128)S(1)}) custom-call(f32[64]{0:T(128)S(1)} %copy-done.9, f32[64]{0:T(128)S(1)} %copy-done.11, f32[64]{0:T(128)S(1)} %copy-done.10, f32[64,7,64,256]{3,2,1,0:T(8,128)} %get-tuple-element.48.pack, f32[31,4,64,256]{3,2,1,0:T(8,128)S(1)} %load.1.window, ...), custom_call_target="tpu_custom_call" | custom-call | flops 41943040 | bytes 14680064 | tf_op jit(solution)/shard_map/pallas_call | solution.py:850
  142.6 3.5 %shard_map.123 = (f32[64,64,256]{2,1,0:T(8,128)}, f32[12,4,64,256]{3,2,1,0:T(8,128)S(1)}, f32[4,64,256]{2,1,0:T(8,128)S(1)}) custom-call(f32[64]{0:T(128)S(1)} %copy-done.9, f32[64]{0:T(128)S(1)} %copy-done.11, f32[64]{0:T(128)S(1)} %copy-done.10, f32[64,7,64,256]{3,2,1,0:T(8,128)} %get-tuple-element.48.pack, ...), custom_call_target="tpu_custom_call", output_to_operand_aliasing={{0}: (14, {})} | custom-call | flops 20971520 | bytes 7340032 | tf_op jit(solution)/shard_map/pallas_call | solution.py:850
  146.1 2.7 %shard_map.124 = (f32[64,64,256]{2,1,0:T(8,128)}, f32[6,4,64,256]{3,2,1,0:T(8,128)S(1)}, f32[4,64,256]{2,1,0:T(8,128)S(1)}) custom-call(f32[64]{0:T(128)S(1)} %copy-done.9, f32[64]{0:T(128)S(1)} %copy-done.11, f32[64]{0:T(128)S(1)} %copy-done.10, f32[64,7,64,256]{3,2,1,0:T(8,128)} %get-tuple-element.48.pack, ...), custom_call_target="tpu_custom_call", output_to_operand_aliasing={{0}: (14, {})} | custom-call | flops 13107200 | bytes 4587520 | tf_op jit(solution)/shard_map/pallas_call | solution.py:850
  148.8 1.8 %shard_map.125 = (f32[64,64,256]{2,1,0:T(8,128)}, f32[5,4,64,256]{3,2,1,0:T(8,128)S(1)}, f32[4,64,256]{2,1,0:T(8,128)S(1)}) custom-call(f32[64]{0:T(128)S(1)} %copy-done.9, f32[64]{0:T(128)S(1)} %copy-done.11, f32[64]{0:T(128)S(1)} %copy-done.10, f32[64,7,64,256]{3,2,1,0:T(8,128)} %get-tuple-element.48.pack, ...), custom_call_target="tpu_custom_call", output_to_operand_aliasing={{0}: (14, {})} | custom-call | flops 5242880 | bytes 1835008 | tf_op jit(solution)/shard_map/pallas_call | solution.py:850
  150.7 2.3 %shard_map.126 = (f32[64,64,256]{2,1,0:T(8,128)}, f32[1,64]{1,0:T(1,128)}) custom-call(f32[64]{0:T(128)S(1)} %copy-done.9, f32[64]{0:T(128)S(1)} %copy-done.11, f32[64]{0:T(128)S(1)} %copy-done.10, f32[64,7,64,256]{3,2,1,0:T(8,128)} %get-tuple-element.48.pack, f32[5,4,64,256]{3,2,1,0:T(8,128)S(1)} %get-tuple-element.73.window, ...), custom_call_target="tpu_custom_call", output_to_operand_aliasing={{0}: (16, {})} | custom-call | flops 2621440 | bytes 917504 | tf_op jit(solution)/shard_map/pallas_call | solution.py:850
  (64 shorter events, 21.1 us)
Async XLA Ops:
  3.5 132.3 %collective-permute-start.10 = (f32[32,64,256]{2,1,0:T(8,128)S(1)}, f32[32,64,256]{2,1,0:T(8,128)S(1)}, u32[]{:S(2)}, u32[]{:S(2)}) collective-permute-start(f32[32,64,256]{2,1,0:T(8,128)S(1)} %head.1), channel_id=1, source_target_pairs={{0,16},{1,17},{2,18},{3,19},{4,20},{5,21},{6,22},{7,23},{8,24},{9,... | collective-permute-start | bytes 6291464 | tf_op jit(solution)/shard_map/ppermute | solution.py:26
  17.0 11.4 %collective-permute-start = (f32[64,256]{1,0:T(8,128)}, f32[64,256]{1,0:T(8,128)S(1)}, u32[]{:S(2)}, u32[]{:S(2)}) collective-permute-start(f32[64,256]{1,0:T(8,128)} %get-tuple-element.41), channel_id=1, source_target_pairs={{0,4},{4,8},{8,12},{1,5},{5,9},{9,13},{2,6},{6,10},{10,14},{3,7},{... | collective-permute-start | bytes 196616 | tf_op jit(solution)/shard_map/ppermute | solution.py:26
  21.5 6.9 %collective-permute-start.1 = (f32[64,256]{1,0:T(8,128)}, f32[64,256]{1,0:T(8,128)S(1)}, u32[]{:S(2)}, u32[]{:S(2)}) collective-permute-start(f32[64,256]{1,0:T(8,128)} %get-tuple-element.42), channel_id=1, source_target_pairs={{4,0},{8,4},{12,8},{5,1},{9,5},{13,9},{6,2},{10,6},{14,10},{7,3},{... | collective-permute-start | bytes 196616 | tf_op jit(solution)/shard_map/ppermute | solution.py:26
  22.8 2.6 %collective-permute-start.2 = (f32[64,128]{1,0:T(8,128)}, f32[64,128]{1,0:T(8,128)S(1)}, u32[]{:S(2)}, u32[]{:S(2)}) collective-permute-start(f32[64,128]{1,0:T(8,128)} %get-tuple-element.43), channel_id=1, source_target_pairs={{0,1},{1,2},{2,3},{4,5},{5,6},{6,7},{8,9},{9,10},{10,11},{12,13},{... | collective-permute-start | bytes 98312 | tf_op jit(solution)/shard_map/ppermute | solution.py:26
  24.1 4.3 %collective-permute-start.3 = (f32[64,128]{1,0:T(8,128)}, f32[64,128]{1,0:T(8,128)S(1)}, u32[]{:S(2)}, u32[]{:S(2)}) collective-permute-start(f32[64,128]{1,0:T(8,128)} %get-tuple-element.44), channel_id=1, source_target_pairs={{1,0},{2,1},{3,2},{5,4},{6,5},{7,6},{9,8},{10,9},{11,10},{13,12},{... | collective-permute-start | bytes 98312 | tf_op jit(solution)/shard_map/ppermute | solution.py:26
  29.1 64.3 %copy-start.5 = (f32[64,256]{1,0:T(8,128)S(1)}, f32[64,256]{1,0:T(8,128)}, u32[]{:S(2)}) copy-start(f32[64,256]{1,0:T(8,128)} %get-tuple-element.54.cu0) | copy-start | bytes 196612
  29.1 64.3 %copy-start.7 = (f32[64,128]{1,0:T(8,128)S(1)}, f32[64,128]{1,0:T(8,128)}, u32[]{:S(2)}) copy-start(f32[64,128]{1,0:T(8,128)} %get-tuple-element.55.cv0) | copy-start | bytes 98308
  29.1 64.3 %copy-start.8 = (f32[64,128]{1,0:T(8,128)S(1)}, f32[64,128]{1,0:T(8,128)}, u32[]{:S(2)}) copy-start(f32[64,128]{1,0:T(8,128)} %get-tuple-element.53.vent_rate) | copy-start | bytes 98308
  29.1 64.3 %copy-start.10 = (f32[64]{0:T(128)S(1)}, f32[64]{0:T(128)}, u32[]{:S(2)}) copy-start(f32[64]{0:T(128)} %profile_hbm.11) | copy-start | bytes 772
  45.3 97.4 %collective-permute-start.11 = (f32[16,64,256]{2,1,0:T(8,128)}, f32[16,64,256]{2,1,0:T(8,128)S(1)}, u32[]{:S(2)}, u32[]{:S(2)}) collective-permute-start(f32[16,64,256]{2,1,0:T(8,128)} %get-tuple-element.62), channel_id=1, source_target_pairs={{0,16},{1,17},{2,18},{3,19},{4,20},{5,21},{6,22},{7,23},{8,24},{9,... | collective-permute-start | bytes 3145736 | tf_op jit(solution)/shard_map/ppermute | solution.py:26
  46.6 99.5 %collective-permute-start.12 = (f32[10,64,256]{2,1,0:T(8,128)}, f32[10,64,256]{2,1,0:T(8,128)S(1)}, u32[]{:S(2)}, u32[]{:S(2)}) collective-permute-start(f32[10,64,256]{2,1,0:T(8,128)} %get-tuple-element.66), channel_id=1, source_target_pairs={{0,16},{1,17},{2,18},{3,19},{4,20},{5,21},{6,22},{7,23},{8,24},{9,... | collective-permute-start | bytes 1966088 | tf_op jit(solution)/shard_map/ppermute | solution.py:26
  48.0 45.4 %collective-permute-start.4 = (f32[160,256]{1,0:T(8,128)}, f32[160,256]{1,0:T(8,128)S(1)}, u32[]{:S(2)}, u32[]{:S(2)}) collective-permute-start(f32[160,256]{1,0:T(8,128)} %get-tuple-element.49.mine), channel_id=1, source_target_pairs={{0,16},{1,17},{2,18},{3,19},{4,20},{5,21},{6,22},{7,23},{8,24},{9,... | collective-permute-start | bytes 491528 | tf_op jit(solution)/shard_map/ppermute | solution.py:26
  49.3 6.4 %collective-permute-start.5 = (f32[64,256]{1,0:T(8,128)}, f32[64,256]{1,0:T(8,128)S(1)}, u32[]{:S(2)}, u32[]{:S(2)}) collective-permute-start(f32[64,256]{1,0:T(8,128)} %get-tuple-element.50.my_vents), channel_id=1, source_target_pairs={{16,0},{17,1},{18,2},{19,3},{20,4},{21,5},{22,6},{23,7},{24,8},{25... | collective-permute-start | bytes 196616 | tf_op jit(solution)/shard_map/ppermute | solution.py:26
  95.3 3.0 %collective-permute-start.15 = (f32[1,64]{1,0:T(1,128)S(1)}, f32[1,64]{1,0:T(1,128)S(1)}, u32[]{:S(2)}, u32[]{:S(2)}) collective-permute-start(f32[1,64]{1,0:T(1,128)S(1)} %get-tuple-element.75), channel_id=1, source_target_pairs={{0,1},{1,0},{2,3},{3,2},{4,5},{5,4},{6,7},{7,6},{8,9},{9,8},{10,11... | collective-permute-start | bytes 776 | tf_op jit(solution)/shard_map/ppermute | solution.py:40
  98.4 5.5 %collective-permute-start.16 = (f32[1,64]{1,0:T(1,128)S(1)}, f32[1,64]{1,0:T(1,128)S(1)}, u32[]{:S(2)}, u32[]{:S(2)}) collective-permute-start(f32[1,64]{1,0:T(1,128)S(1)} %add.12), channel_id=1, source_target_pairs={{0,2},{1,3},{2,0},{3,1},{4,6},{5,7},{6,4},{7,5},{8,10},{9,11},{10,... | collective-permute-start | bytes 776 | tf_op jit(solution)/shard_map/ppermute | solution.py:40
  103.8 5.5 %collective-permute-start.17 = (f32[1,64]{1,0:T(1,128)S(1)}, f32[1,64]{1,0:T(1,128)S(1)}, u32[]{:S(2)}, u32[]{:S(2)}) collective-permute-start(f32[1,64]{1,0:T(1,128)S(1)} %add.13), channel_id=1, source_target_pairs={{0,4},{1,5},{2,6},{3,7},{4,0},{5,1},{6,2},{7,3},{8,12},{9,13},{10,... | collective-permute-start | bytes 776 | tf_op jit(solution)/shard_map/ppermute | solution.py:40
  107.3 9.6 %collective-permute-start.8 = (f32[64,128]{1,0:T(8,128)S(1)}, f32[64,128]{1,0:T(8,128)S(1)}, u32[]{:S(2)}, u32[]{:S(2)}) collective-permute-start(f32[64,128]{1,0:T(8,128)S(1)} %get-tuple-element.58), channel_id=1, source_target_pairs={{0,1},{1,2},{2,3},{4,5},{5,6},{6,7},{8,9},{9,10},{10,11},{12,13},{... | collective-permute-start | bytes 98312 | tf_op jit(solution)/shard_map/ppermute | solution.py:26
  109.3 6.3 %collective-permute-start.18 = (f32[1,64]{1,0:T(1,128)S(1)}, f32[1,64]{1,0:T(1,128)S(1)}, u32[]{:S(2)}, u32[]{:S(2)}) collective-permute-start(f32[1,64]{1,0:T(1,128)S(1)} %add.14), channel_id=1, source_target_pairs={{0,8},{1,9},{2,10},{3,11},{4,12},{5,13},{6,14},{7,15},{8,0},{9,1},... | collective-permute-start | bytes 776 | tf_op jit(solution)/shard_map/ppermute | solution.py:40
  115.6 3.1 %collective-permute-start.9 = (f32[64,128]{1,0:T(8,128)S(1)}, f32[64,128]{1,0:T(8,128)S(1)}, u32[]{:S(2)}, u32[]{:S(2)}) collective-permute-start(f32[64,128]{1,0:T(8,128)S(1)} %get-tuple-element.59), channel_id=1, source_target_pairs={{1,0},{2,1},{3,2},{5,4},{6,5},{7,6},{9,8},{10,9},{11,10},{13,12},{... | collective-permute-start | bytes 98312 | tf_op jit(solution)/shard_map/ppermute | solution.py:26
  116.9 31.9 %collective-permute-start.13 = (f32[4,64,256]{2,1,0:T(8,128)}, f32[4,64,256]{2,1,0:T(8,128)S(1)}, u32[]{:S(2)}, u32[]{:S(2)}) collective-permute-start(f32[4,64,256]{2,1,0:T(8,128)} %get-tuple-element.70), channel_id=1, source_target_pairs={{0,16},{1,17},{2,18},{3,19},{4,20},{5,21},{6,22},{7,23},{8,24},{9,... | collective-permute-start | bytes 786440 | tf_op jit(solution)/shard_map/ppermute | solution.py:26
  118.7 5.4 %collective-permute-start.6 = (f32[64,256]{1,0:T(8,128)S(1)}, f32[64,256]{1,0:T(8,128)S(1)}, u32[]{:S(2)}, u32[]{:S(2)}) collective-permute-start(f32[64,256]{1,0:T(8,128)S(1)} %get-tuple-element.56), channel_id=1, source_target_pairs={{0,4},{4,8},{8,12},{1,5},{5,9},{9,13},{2,6},{6,10},{10,14},{3,7},{... | collective-permute-start | bytes 196616 | tf_op jit(solution)/shard_map/ppermute | solution.py:26
  124.1 7.0 %collective-permute-start.7 = (f32[64,256]{1,0:T(8,128)S(1)}, f32[64,256]{1,0:T(8,128)S(1)}, u32[]{:S(2)}, u32[]{:S(2)}) collective-permute-start(f32[64,256]{1,0:T(8,128)S(1)} %get-tuple-element.57), channel_id=1, source_target_pairs={{4,0},{8,4},{12,8},{5,1},{9,5},{13,9},{6,2},{10,6},{14,10},{7,3},{... | collective-permute-start | bytes 196616 | tf_op jit(solution)/shard_map/ppermute | solution.py:26
  131.0 19.6 %collective-permute-start.14 = (f32[2,64,256]{2,1,0:T(8,128)}, f32[2,64,256]{2,1,0:T(8,128)S(1)}, u32[]{:S(2)}, u32[]{:S(2)}) collective-permute-start(f32[2,64,256]{2,1,0:T(8,128)} %get-tuple-element.74), channel_id=1, source_target_pairs={{0,16},{1,17},{2,18},{3,19},{4,20},{5,21},{6,22},{7,23},{8,24},{9,... | collective-permute-start | bytes 393224 | tf_op jit(solution)/shard_map/ppermute | solution.py:26
  135.8 14.9 %collective-permute-start.19 = (f32[1,64]{1,0:T(1,128)S(1)}, f32[1,64]{1,0:T(1,128)S(1)}, u32[]{:S(2)}, u32[]{:S(2)}) collective-permute-start(f32[1,64]{1,0:T(1,128)S(1)} %add.15.rest_0_), channel_id=1, source_target_pairs={{0,16},{1,17},{2,18},{3,19},{4,20},{5,21},{6,22},{7,23},{8,24},{9,... | collective-permute-start | bytes 776 | tf_op jit(solution)/shard_map/ppermute | solution.py:26
  (13 other events, 154.9 us)
